TPU v7x, 512 devices: a whole 4x8x8 slice. The times are simulated.
512 devices in a mesh: ctx: 32 (over y, x_lo, core), head: 16 (over z, x_hi).
Axes of the slice: x: 4 (x_hi: 2, x_lo: 2; x = x_hi * 2 + x_lo), y: 8, z: 8, core: 2. Of those that a mesh axis runs over, the one named last changes fastest.
Arguments:
- query_in: bfloat16 [4096, 4096], P(('ctx', 'head')), may hold values from -20 to 20
- key_in: bfloat16 [4096, 4096], P('ctx', 'head'), may hold values from -20 to 20
- value_in: bfloat16 [4096, 4096], P('ctx', 'head'), may hold values from -6 to 6
- out_saved: bfloat16 [4096, 4096], P(('ctx', 'head')), may hold values from -1.5 to 1.5
- out_grad: bfloat16 [4096, 4096], P(('ctx', 'head')), may hold values from -24 to 24
- span_place: int32 [64], replicated, may hold values from 0 to 63, each once
Outputs:
- grad_query: bfloat16 [4096, 4096], P(('ctx', 'head'))
- grad_key: bfloat16 [4096, 4096], P('ctx', 'head')
- grad_value: bfloat16 [4096, 4096], P('ctx', 'head')
Inputs may be any that keep to these rules, and one draw needn't show every extreme that they name: `span_place`: each block position appears once.
All inputs are finite; a program needn't handle non-finite values.
Results may differ from a plain program's by a relative error of at most 0.0049.
Values may be sent and summed in bfloat16 or wider, within the bound.
No kernel may reach another device: no remote copies, remote signals or barrier semaphores. Data moves between devices by JAX's collectives and lax.ppermute only.
A program may use at most 64 MiB of HBM per device.

v0:
```python
import jax
import jax.numpy as jnp
from jax import lax
from jax.sharding import Mesh
from jax.sharding import PartitionSpec as P

HEAD_DIM = 128
HEAD = ("head_0", "head_1")
CTX_HEAD = ("ctx", "head_0", "head_1")


def split_up(x, dim, peers):
    before, after = (x.shape[:dim], x.shape[dim + 1 :])
    return jnp.moveaxis(x.reshape(*before, peers, -1, *after), dim, 0)


def in_order(tiles, dim):
    tiles = jnp.moveaxis(tiles, 0, dim)
    lengths = tiles.shape
    return tiles.reshape(*lengths[:dim], lengths[dim] * lengths[dim + 1], *lengths[dim + 2 :])


def moved_by_axis(tiles, axes, order):
    lengths = [lax.axis_size(a) for a in axes]
    tiles = tiles.reshape(*lengths, *tiles.shape[1:])
    for k in order:
        tiles = lax.all_to_all(tiles, axes[k], split_axis=k, concat_axis=k, tiled=True)
    return tiles.reshape(-1, *tiles.shape[len(axes) :])


def exchange_by_axis(x, axes, order, split_dim, concat_dim):
    tiles = split_up(x, split_dim, lax.axis_size(axes))
    return in_order(moved_by_axis(tiles, axes, order), concat_dim)


def side_by_side(arrays, axis, dim, along):
    ends, at = ([], 0)
    for a in arrays[:-1]:
        at += a.shape[along]
        ends.append(at)
    both = jnp.concatenate(arrays, axis=along)
    return tuple(jnp.split(lax.all_gather(both, axis, axis=dim, tiled=True), ends, axis=along))


def sent_together(arrays, axis, split_dim, concat_dim, along):
    both = jnp.concatenate(arrays, axis=along)
    whole, at, gathered = (
        lax.all_to_all(both, axis, split_axis=split_dim, concat_axis=concat_dim, tiled=True),
        0,
        [],
    )
    for a in arrays:
        gathered.append(lax.slice_in_dim(whole, at, at + a.shape[along], axis=along))
        at += a.shape[along]
    return tuple(gathered)


def positions_of(span_place, first, count, span_len):
    index = first + jnp.arange(count, dtype=jnp.int32)
    span_id = index // span_len
    table = jnp.arange(span_place.shape[0], dtype=jnp.int32)
    place = jnp.sum(jnp.where(span_id[:, None] == table[None, :], span_place[None, :], 0), axis=1)
    return place * span_len + index % span_len


def heads_view(block):
    return block.reshape(block.shape[0], block.shape[1] // HEAD_DIM, HEAD_DIM)


def block_grads(
    query_part, grad_part, lse_part, delta_part, query_pos, key_part, value_part, key_pos
):
    scale = HEAD_DIM ** (-0.5)
    query_heads = heads_view(query_part)
    grad_heads = heads_view(grad_part)
    key_heads = heads_view(key_part)
    value_heads = heads_view(value_part)
    scores = (
        jnp.einsum("rhd,thd->hrt", query_heads, key_heads, preferred_element_type=jnp.float32)
        * scale
    )
    visible = key_pos[None, None, :] <= query_pos[None, :, None]
    probs = jnp.exp(jnp.where(visible, scores - lse_part[:, :, None], -jnp.inf))
    dprobs = jnp.einsum("rhd,thd->hrt", grad_heads, value_heads, preferred_element_type=jnp.float32)
    dscores = (probs * (dprobs - delta_part[:, :, None]) * scale).astype(jnp.bfloat16)
    grad_q = jnp.einsum("hrt,thd->rhd", dscores, key_heads, preferred_element_type=jnp.float32)
    grad_k = jnp.einsum("hrt,rhd->thd", dscores, query_heads, preferred_element_type=jnp.float32)
    grad_v = jnp.einsum(
        "hrt,rhd->thd", probs.astype(jnp.bfloat16), grad_heads, preferred_element_type=jnp.float32
    )
    return (
        grad_q.reshape(query_part.shape),
        grad_k.reshape(key_part.shape),
        grad_v.reshape(key_part.shape),
    )


def body(query_in, key_in, value_in, out_saved, out_grad, span_place):
    cycle_size = lax.axis_size("ctx")
    my_index = lax.axis_index("ctx")
    row_count = key_in.shape[0]
    span_len = row_count // 2
    feature_width = key_in.shape[1]
    group = feature_width // HEAD_DIM
    scale = HEAD_DIM ** (-0.5)
    token_rows = query_in.shape[0]
    all_heads = query_in.shape[1] // HEAD_DIM
    products = out_grad.astype(jnp.float32) * out_saved.astype(jnp.float32)
    delta_tokens = jnp.sum(products.reshape(token_rows, all_heads, HEAD_DIM), axis=2)
    query_local, grad_local = (
        exchange_by_axis(query_in, HEAD, (0, 1), 1, 0),
        exchange_by_axis(out_grad, HEAD, (0, 1), 1, 0),
    )
    delta_rows = lax.all_to_all(delta_tokens, HEAD, split_axis=1, concat_axis=0, tiled=True)
    delta_local = delta_rows.T
    my_pos = positions_of(span_place, my_index * row_count, row_count, span_len)
    query_heads = heads_view(query_local)

    def stat_step(carry, piece, start):
        top, total = carry
        key_pos = positions_of(span_place, start, piece.shape[0], span_len)
        scores = (
            jnp.einsum(
                "rhd,thd->hrt", query_heads, heads_view(piece), preferred_element_type=jnp.float32
            )
            * scale
        )
        visible = key_pos[None, None, :] <= my_pos[None, :, None]
        masked = jnp.where(visible, scores, -jnp.inf)
        new_top = jnp.maximum(top, jnp.max(masked, axis=2))
        total = total * jnp.exp(top - new_top) + jnp.sum(
            jnp.exp(masked - new_top[:, :, None]), axis=2
        )
        return (new_top, total)

    start_top = jnp.full((group, row_count), -1e30, jnp.float32)
    start_total = jnp.zeros((group, row_count), jnp.float32)
    zeros_rows = jnp.zeros((row_count, feature_width), jnp.float32)
    key_all, value_all = side_by_side((key_in, value_in), "ctx", 0, 1)
    total_rows = key_all.shape[0]
    block_count = max(cycle_size // 8, 1)
    block_rows = total_rows // block_count
    key_blocks = key_all.reshape(block_count, block_rows, feature_width)
    value_blocks = value_all.reshape(block_count, block_rows, feature_width)
    block_starts = jnp.arange(block_count, dtype=jnp.int32) * block_rows

    def stat_scan(carry, block):
        piece, first = block
        return (stat_step(carry, piece, first), None)

    stats, unused = lax.scan(stat_scan, (start_top, start_total), (key_blocks, block_starts))
    lse_local = stats[0] + jnp.log(stats[1])

    def grad_scan(grad_q, block):
        key_block, value_block, first = block
        key_pos = positions_of(span_place, first, block_rows, span_len)
        part_q, part_k, part_v = block_grads(
            query_local, grad_local, lse_local, delta_local, my_pos, key_block, value_block, key_pos
        )
        return (grad_q + part_q, (part_k, part_v))

    grad_q, partials = lax.scan(grad_scan, zeros_rows, (key_blocks, value_blocks, block_starts))
    stacked_k = partials[0].reshape(cycle_size, row_count, feature_width)
    stacked_v = partials[1].reshape(cycle_size, row_count, feature_width)
    home_k, home_v = sent_together((stacked_k, stacked_v), "ctx", 0, 0, 1)
    grad_k = jnp.sum(home_k, axis=0)
    grad_v = jnp.sum(home_v, axis=0)
    grad_query = lax.all_to_all(
        grad_q.astype(jnp.bfloat16), HEAD, split_axis=0, concat_axis=1, tiled=True
    )
    return (grad_query, grad_k.astype(jnp.bfloat16), grad_v.astype(jnp.bfloat16))


def solution(mesh):
    torus = Mesh(mesh.devices.reshape(mesh.shape["ctx"], 8, 2), ("ctx", "head_0", "head_1"))
    return jax.shard_map(
        body,
        mesh=torus,
        in_specs=(
            P(CTX_HEAD, None),
            P("ctx", HEAD),
            P("ctx", HEAD),
            P(CTX_HEAD, None),
            P(CTX_HEAD, None),
            P(),
        ),
        out_specs=(P(CTX_HEAD, None), P("ctx", HEAD), P("ctx", HEAD)),
        check_vma=False,
    )
```

profile of v0, /device:TPU:1, one launch (start us, length us, event | category | flops | bytes accessed | tf_op | source)
XLA Modules:
  0.0 374.9 jit_solution(13385605163741970954)
XLA Ops:
  9.8 22.1 %all_to_all.63 = f32[8,16,2]{0,2,1:T(2,128)S(1)} all-to-all(f32[8,16,2]{0,2,1:T(2,128)S(1)} %bitcast.147), channel_id=1, replica_groups=mesh['ctx'=32,'head_0'=8,'head_1'=2] {'head_0','head_1'}, dimensions={1} | all-to-all | bytes 2048 | tf_op jit(solution)/shard_map/all_to_all | solution.py:114
  31.9 3.4 all-to-all-start
  35.3 7.1 %all-to-all-done = bf16[8,2,8,256]{3,2,1,0:T(8,128)(2,1)S(1)} async-done(((bf16[8,2,8,256]{3,2,1,0:T(8,128)(2,1)}), bf16[8,2,8,256]{3,2,1,0:T(8,128)(2,1)S(1)}, u32[]{:S(2)}, u32[]{:S(2)}) %all-to-all-start) | async-done | bytes 65568 | tf_op jit(solution)/shard_map/all_to_all | solution.py:27
  42.4 3.4 all-to-all-start.2
  47.2 5.7 %all-to-all-done.2 = bf16[8,2,8,256]{3,2,1,0:T(8,128)(2,1)S(1)} async-done(((bf16[8,2,8,256]{3,2,1,0:T(8,128)(2,1)}), bf16[8,2,8,256]{3,2,1,0:T(8,128)(2,1)S(1)}, u32[]{:S(2)}, u32[]{:S(2)}) %all-to-all-start.2) | async-done | bytes 65568 | tf_op jit(solution)/shard_map/all_to_all | solution.py:27
  52.9 3.3 all-to-all-start.1
  56.9 4.4 %all-to-all-done.1 = bf16[8,2,8,256]{3,2,0,1:T(8,128)(2,1)S(1)} async-done(((bf16[8,2,8,256]{3,2,0,1:T(8,128)(2,1)}), bf16[8,2,8,256]{3,2,0,1:T(8,128)(2,1)S(1)}, u32[]{:S(2)}, u32[]{:S(2)}) %all-to-all-start.1) | async-done | bytes 65568 | tf_op jit(solution)/shard_map/all_to_all | solution.py:27
  61.3 3.3 all-to-all-start.3
  64.8 4.2 %all-to-all-done.3 = bf16[8,2,8,256]{3,2,0,1:T(8,128)(2,1)S(1)} async-done(((bf16[8,2,8,256]{3,2,0,1:T(8,128)(2,1)}), bf16[8,2,8,256]{3,2,0,1:T(8,128)(2,1)S(1)}, u32[]{:S(2)}, u32[]{:S(2)}) %all-to-all-start.3) | async-done | bytes 65568 | tf_op jit(solution)/shard_map/all_to_all | solution.py:27
  69.1 16.1 %all-gather.2.cloned.1.call-done = bf16[4096,512]{1,0:T(8,128)(2,1)} async-done(((bf16[128,512]{1,0:T(8,128)(2,1)}), bf16[4096,512]{1,0:T(8,128)(2,1)}) %all-gather.2.cloned.1.call-update) | async-done | bytes 4194320 | tf_op jit(solution)/shard_map/all_gather | solution.py:42
  85.2 3.8 %fusion.28 = (bf16[4096,256]{1,0:T(8,128)(2,1)}, bf16[4096,256]{1,0:T(8,128)(2,1)S(1)}) fusion(bf16[4096,512]{1,0:T(8,128)(2,1)} %all-gather.2.cloned.1.call-done), kind=kLoop, calls=%fused_computation.76 | loop fusion | bytes 8388608 | tf_op jit(solution)/shard_map/split | solution.py:42
  89.1 2.5 copy.112
  91.5 14.8 %while.33 = (s32[]{:T(128)}, f32[2,128]{1,0:T(2,128)S(1)}, f32[2,128]{1,0:T(2,128)S(1)}, s32[4]{0:T(128)S(1)}, s32[64]{0:T(128)S(1)}, /*index=5*/s32[128]{0:T(12...) while((s32[]{:T(128)}, f32[2,128]{1,0:T(2,128)S(1)}, ...), condition=%wide.region_5.6_spmd.clone, body=%wide.region_1.0_spmd.clone.sunk | while | flops 68778240 | bytes 4036496 | solution.py:151
  106.4 43.0 %while.34 = (s32[]{:T(128)}, f32[128,256]{0,1:T(8,128)S(1)}, f32[4,1024,256]{2,1,0:T(8,128)}, f32[4,1024,256]{2,1,0:T(8,128)}, bf16[4,1024,256]{1,2,0:T(8,128)(2...) while((s32[]{:T(128)}, f32[128,256]{0,1:T(8,128)S(1)}, ...), condition=%wide.wide.region_9.10_spmd.clone, body=%wide.wide.region_7.9_spmd.clone.sunk | while | flops 338064384 | bytes 21261264 | solution.py:162
  114.2 1.6 copy.147
  125.0 1.6 copy.147
  135.7 1.6 copy.147
  146.5 1.6 copy.147
  150.2 9.0 %all-to-all-start.5 = ((bf16[16,8,256]{2,1,0:T(8,128)(2,1)}), bf16[16,8,256]{2,1,0:T(8,128)(2,1)S(1)}, u32[]{:S(2)}, u32[]{:S(2)}) async-start(bf16[16,8,256]{2,1,0:T(8,128)(2,1)} %bitcast.65), calls=%async_computation.5 | async-start | bytes 131072 | tf_op jit(solution)/shard_map/all_to_all | solution.py:168
  159.2 7.6 %pad_maximum_fusion = f32[32,256,256]{2,1,0:T(8,128)} fusion(f32[32,128,256]{2,1,0:T(8,128)} %bitcast.143, f32[32,128,256]{2,1,0:T(8,128)} %bitcast.144), kind=kLoop, calls=%fused_computation.58 | loop fusion | flops 2097152 | bytes 16777216 | tf_op jit(solution)/shard_map/concatenate | solution.py:46
  166.8 1.8 all-to-all-done.5
  168.6 7.7 %all-to-all-start.6 = ((f32[32,256,256]{2,1,0:T(8,128)}), f32[32,256,256]{2,1,0:T(8,128)}, u32[]{:S(2)}, u32[]{:S(2)}) async-start(f32[32,256,256]{2,1,0:T(8,128)} %pad_maximum_fusion), calls=%async_computation.6 | async-start | bytes 16777216 | tf_op jit(solution)/shard_map/all_to_all | solution.py:48
  176.3 186.5 %all-to-all-done.6 = f32[32,256,256]{2,1,0:T(8,128)} async-done(((f32[32,256,256]{2,1,0:T(8,128)}), f32[32,256,256]{2,1,0:T(8,128)}, u32[]{:S(2)}, u32[]{:S(2)}) %all-to-all-start.6) | async-done | bytes 8388640 | tf_op jit(solution)/shard_map/all_to_all | solution.py:48
  362.7 4.7 %slice_reduce_fusion = (bf16[128,256]{1,0:T(8,128)(2,1)}, bf16[128,256]{1,0:T(8,128)(2,1)}) fusion(f32[32,256,256]{2,1,0:T(8,128)} %all-to-all-done.6), kind=kLoop, calls=%fused_computation.59 | loop fusion | flops 2031616 | bytes 8519680 | tf_op jit(solution)/shard_map/reduce_sum | solution.py:167
  (148 shorter events, 57.2 us)
Async XLA Ops:
  7.2 78.1 %all-gather.2.cloned.1.call-start = ((), (), s32[]{:S(2)}) async-start(), calls=%async_computation.7 | async-start | bytes 4325376 | tf_op jit(solution)/shard_map/all_gather | solution.py:42
  31.9 10.5 %all-to-all-start = ((bf16[8,2,8,256]{3,2,1,0:T(8,128)(2,1)}), bf16[8,2,8,256]{3,2,1,0:T(8,128)(2,1)S(1)}, u32[]{:S(2)}, u32[]{:S(2)}) async-start(bf16[8,2,8,256]{3,2,1,0:T(8,128)(2,1)} %bitcast.148), calls=%async_computation | async-start | bytes 131072 | tf_op jit(solution)/shard_map/all_to_all | solution.py:27
  42.4 10.5 %all-to-all-start.2 = ((bf16[8,2,8,256]{3,2,1,0:T(8,128)(2,1)}), bf16[8,2,8,256]{3,2,1,0:T(8,128)(2,1)S(1)}, u32[]{:S(2)}, u32[]{:S(2)}) async-start(bf16[8,2,8,256]{3,2,1,0:T(8,128)(2,1)} %bitcast.145), calls=%async_computation.2 | async-start | bytes 131072 | tf_op jit(solution)/shard_map/all_to_all | solution.py:27
  52.9 8.4 %all-to-all-start.1 = ((bf16[8,2,8,256]{3,2,0,1:T(8,128)(2,1)}), bf16[8,2,8,256]{3,2,0,1:T(8,128)(2,1)S(1)}, u32[]{:S(2)}, u32[]{:S(2)}) async-start(bf16[8,2,8,256]{3,2,0,1:T(8,128)(2,1)} %copy.106), calls=%async_computation.1 | async-start | bytes 131072 | tf_op jit(solution)/shard_map/all_to_all | solution.py:27
  61.3 7.8 %all-to-all-start.3 = ((bf16[8,2,8,256]{3,2,0,1:T(8,128)(2,1)}), bf16[8,2,8,256]{3,2,0,1:T(8,128)(2,1)S(1)}, u32[]{:S(2)}, u32[]{:S(2)}) async-start(bf16[8,2,8,256]{3,2,0,1:T(8,128)(2,1)} %copy.110), calls=%async_computation.3 | async-start | bytes 131072 | tf_op jit(solution)/shard_map/all_to_all | solution.py:27
  64.8 24.3 %copy-start = (bf16[8,2,8,256]{3,2,1,0:T(8,128)(2,1)}, bf16[8,2,8,256]{3,2,1,0:T(8,128)(2,1)S(1)}, u32[]{:S(2)}) copy-start(bf16[8,2,8,256]{3,2,1,0:T(8,128)(2,1)S(1)} %copy.113) | copy-start | bytes 196612
  69.1 20.0 %copy-start.1 = (bf16[8,2,8,256]{3,2,1,0:T(8,128)(2,1)}, bf16[8,2,8,256]{3,2,1,0:T(8,128)(2,1)S(1)}, u32[]{:S(2)}) copy-start(bf16[8,2,8,256]{3,2,1,0:T(8,128)(2,1)S(1)} %copy.115) | copy-start | bytes 196612
  89.1 2.5 copy-start.2
  150.2 18.4 %all-to-all-start.5 = ((bf16[16,8,256]{2,1,0:T(8,128)(2,1)}), bf16[16,8,256]{2,1,0:T(8,128)(2,1)S(1)}, u32[]{:S(2)}, u32[]{:S(2)}) async-start(bf16[16,8,256]{2,1,0:T(8,128)(2,1)} %bitcast.65), calls=%async_computation.5 | async-start | bytes 131072 | tf_op jit(solution)/shard_map/all_to_all | solution.py:168
  168.6 194.1 %all-to-all-start.6 = ((f32[32,256,256]{2,1,0:T(8,128)}), f32[32,256,256]{2,1,0:T(8,128)}, u32[]{:S(2)}, u32[]{:S(2)}) async-start(f32[32,256,256]{2,1,0:T(8,128)} %pad_maximum_fusion), calls=%async_computation.6 | async-start | bytes 16777216 | tf_op jit(solution)/shard_map/all_to_all | solution.py:48
Sparse Core Ops, SparseCore 0:
  10.1 75.0 all-gather.1
where the time goes:
time: 376 us; the launch traced here: 375 us
  waiting for transfers between devices  226 us (60%)
  local copies, waits for them, and re-layouts  41.9 us (11%)
  starting transfers between devices  30 us (8%)
  other arithmetic  28 us (7%)
  blocking collectives  22.1 us (6%)
  between operations  14.2 us (4%)
  matrix products  12 us (3%)
    all_to_all x1, waiting for transfers between devices, sent_together(): lax.all_to_all(both, axis, split_axis=split_dim, concat_axis=concat_dim,...  186 us
    all_to_all x1, blocking collectives, body(): lax.all_to_all(delta_tokens, HEAD, split_axis=1, concat_axis=0, tiled=True)  22.1 us
    all_to_all x4, waiting for transfers between devices, moved_by_axis(): lax.all_to_all(tiles, axes[k], split_axis=k, concat_axis=k, tiled=True)  21.6 us
    dynamic_slice x24, local copies, waits for them, and re-layouts, body(): lax.scan(stat_scan, (start_top, start_total), (key_blocks, block_starts))  18.4 us
    all_gather x1, waiting for transfers between devices, side_by_side(): lax.all_gather(both, axis, axis=dim, tiled=True)  16.1 us
    dynamic_update_slice x12, local copies, waits for them, and re-layouts, body(): lax.scan(grad_scan, zeros_rows, (key_blocks, value_blocks, block_starts))  13.4 us
    all_to_all x4, starting transfers between devices, moved_by_axis(): lax.all_to_all(tiles, axes[k], split_axis=k, concat_axis=k, tiled=True)  13.3 us
    all_to_all x1, starting transfers between devices, body(): lax.all_to_all(grad_q.astype(jnp.bfloat16), HEAD, split_axis=0, concat_ax...  9 us
  transfers between devices with their start and end apart: 7, of which 7 were waited for; matrix products, arithmetic and copies ran while one was open for 3% of the time, Pallas kernels for 0%

commit v1 on v0

v1 whole, which is shorter than its diff:
```python
import jax
import jax.numpy as jnp
from jax import lax
from jax.experimental import pallas as pl
from jax.experimental.pallas import tpu as pltpu
from jax.sharding import Mesh
from jax.sharding import PartitionSpec as P

HEAD_DIM = 128
SCALE = HEAD_DIM ** (-0.5)
SPAN = 64
HEADS_AXES = ("z", "xh", "c")
KV_AXES = ("yl", "xl", "c")
Q_AXES = ("yh",)
CTX_HEAD = ("yh", "yl", "xl", "c", "z", "xh")
CTX = ("yh", "yl", "xl", "c")
HEAD = ("z", "xh")
NEG = -1e30


def key_positions(place_ref, out_ref):
    first = lax.axis_index("yh") * 16
    row = lax.broadcasted_iota(jnp.int32, (SPAN, HEAD_DIM), 0)
    for s in range(16):
        out_ref[s * SPAN : (s + 1) * SPAN, :] = row + place_ref[first + s] * SPAN


def query_positions(place_ref, b):
    chip = (b * 2 + lax.axis_index("yl")) * 2 + lax.axis_index("xl")
    lane = lax.broadcasted_iota(jnp.int32, (1, 256), 1)
    core_one = ((lane // 8) % 2) == 1
    late = lane >= 128
    at = [[place_ref[chip * 4 + c * 2 + k] for k in range(2)] for c in range(2)]
    place = jnp.where(
        core_one,
        jnp.where(late, at[1][1], at[1][0]),
        jnp.where(late, at[0][1], at[0][0]),
    )
    return place * SPAN + ((lane // 16) % 8) * 8 + lane % 8


def rows_of(ref, b, k):
    return ref[b, :, k].astype(jnp.float32).reshape(256, HEAD_DIM).astype(jnp.bfloat16)


def dot(a, b, dims):
    return lax.dot_general(a, b, (dims, ((), ())), preferred_element_type=jnp.float32)


def stats_kernel(place_ref, own_ref, q_ref, kv_ref, out_ref, kpos_ref):
    key_positions(place_ref, kpos_ref)
    grad = own_ref[:, 1].astype(jnp.float32).reshape(256, HEAD_DIM)
    saved = own_ref[:, 2].astype(jnp.float32).reshape(256, HEAD_DIM)
    delta = jnp.sum((grad * saved).T, axis=0, keepdims=True)
    keys = kv_ref[:, :128].reshape(1024, HEAD_DIM)
    kpos = jnp.concatenate([kpos_ref[...]] * 2, axis=1)
    zeros = jnp.zeros((6, HEAD_DIM), jnp.float32)
    tops, totals = [], []
    for b in range(4):
        scores = dot(keys, rows_of(q_ref, b, 0), ((1,), (1,))) * SCALE
        scores = jnp.where(kpos <= query_positions(place_ref, b), scores, -jnp.inf)
        top = jnp.maximum(jnp.max(scores, axis=0, keepdims=True), NEG)
        total = jnp.sum(jnp.exp(scores - top), axis=0, keepdims=True)
        for k in range(2):
            tops.append(top[:, k * 128 : (k + 1) * 128])
            totals.append(total[:, k * 128 : (k + 1) * 128])
    block = jnp.concatenate(
        tops + totals + [delta[:, :128], delta[:, 128:], zeros], axis=0
    )
    for p in range(4):
        out_ref[p] = block


def grads_kernel(place_ref, stats_ref, q_ref, kv_ref, dq_ref, dkv_ref, kpos_ref, acc_ref):
    key_positions(place_ref, kpos_ref)
    top = jnp.max(stats_ref[:, 0:8], axis=0)
    total = jnp.zeros((8, HEAD_DIM), jnp.float32)
    for p in range(4):
        total += stats_ref[p, 8:16] * jnp.exp(stats_ref[p, 0:8] - top)
    lse8 = top + jnp.log(total)
    lse = jnp.concatenate([lse8[j : j + 1] for j in range(8)], axis=1)
    delta = jnp.concatenate(
        [stats_ref[b, 16 + k : 17 + k] for b in range(4) for k in range(2)], axis=1
    )
    qpos = jnp.concatenate([query_positions(place_ref, b) for b in range(4)], axis=1)
    queries = jnp.concatenate([rows_of(q_ref, b, 0) for b in range(4)], axis=0)
    grads = jnp.concatenate([rows_of(q_ref, b, 1) for b in range(4)], axis=0)
    for j in range(8):
        keys = kv_ref[j, :128]
        values = kv_ref[j, 128:]
        kpos = jnp.concatenate([kpos_ref[j * 128 : (j + 1) * 128, :]] * 8, axis=1)
        scores = dot(keys, queries, ((1,), (1,))) * SCALE
        probs = jnp.exp(jnp.where(kpos <= qpos, scores - lse, -jnp.inf))
        dprobs = dot(values, grads, ((1,), (1,)))
        dscores = (probs * (dprobs - delta) * SCALE).astype(jnp.bfloat16)
        dkv_ref[j, :128] = dot(dscores, queries, ((1,), (0,))).astype(jnp.bfloat16)
        dkv_ref[j, 128:] = dot(probs.astype(jnp.bfloat16), grads, ((1,), (0,))).astype(jnp.bfloat16)
        part = dot(keys.T, dscores, ((1,), (0,)))
        if j == 0:
            acc_ref[...] = part
        else:
            acc_ref[...] += part
    for b in range(4):
        dq_ref[b] = acc_ref[:, b * 256 : (b + 1) * 256].T.astype(jnp.bfloat16)


def kv_pack_kernel(key_ref, value_ref, out_ref):
    for c in range(2):
        block = jnp.concatenate(
            [key_ref[:, c * 128 : (c + 1) * 128], value_ref[:, c * 128 : (c + 1) * 128]], axis=0
        )
        for p in range(4):
            out_ref[p * 2 + c] = block


def q_pack_kernel(own_ref, out_ref):
    block = own_ref[:, :2]
    for p in range(4):
        out_ref[p] = block


def dq_sum_kernel(parts_ref, out_ref):
    total = parts_ref[0].astype(jnp.float32)
    for p in range(1, 4):
        total += parts_ref[p].astype(jnp.float32)
    out_ref[...] = total.astype(jnp.bfloat16)


def dkv_sum_kernel(parts_ref, dk_ref, dv_ref):
    for c in range(2):
        total = parts_ref[c].astype(jnp.float32)
        for p in range(1, 4):
            total += parts_ref[p * 2 + c].astype(jnp.float32)
        total = total.astype(jnp.bfloat16)
        dk_ref[:, c * 128 : (c + 1) * 128] = total[:128]
        dv_ref[:, c * 128 : (c + 1) * 128] = total[128:]


VMEM = pl.BlockSpec(memory_space=pltpu.VMEM)
SMEM = pl.BlockSpec(memory_space=pltpu.SMEM)


def head_tiles(x):
    return x.reshape(8, 32, HEAD_DIM).transpose(1, 0, 2)


def body(query_in, key_in, value_in, out_saved, out_grad, span_place):
    mine = jnp.stack([head_tiles(query_in), head_tiles(out_grad), head_tiles(out_saved)], axis=1)
    own = lax.all_to_all(mine, HEADS_AXES, 0, 0, tiled=True)
    q_send = pl.pallas_call(
        q_pack_kernel,
        out_shape=jax.ShapeDtypeStruct((4, 32, 2, 8, HEAD_DIM), jnp.bfloat16),
        in_specs=[VMEM],
        out_specs=VMEM,
        name="q_pack",
    )(own)
    q_all = lax.all_to_all(q_send, Q_AXES, 0, 0, tiled=True)

    kv_send = pl.pallas_call(
        kv_pack_kernel,
        out_shape=jax.ShapeDtypeStruct((8, 256, HEAD_DIM), jnp.bfloat16),
        in_specs=[VMEM, VMEM],
        out_specs=VMEM,
        name="kv_pack",
    )(key_in, value_in)
    kv_all = lax.all_to_all(kv_send, KV_AXES, 0, 0, tiled=True)

    stats = pl.pallas_call(
        stats_kernel,
        out_shape=jax.ShapeDtypeStruct((4, 24, HEAD_DIM), jnp.float32),
        in_specs=[SMEM, VMEM, VMEM, VMEM],
        out_specs=VMEM,
        scratch_shapes=[pltpu.VMEM((1024, HEAD_DIM), jnp.int32)],
        name="stats",
    )(span_place, own, q_all, kv_all)
    stats_all = lax.all_to_all(stats, Q_AXES, 0, 0, tiled=True)

    dq, dkv = pl.pallas_call(
        grads_kernel,
        out_shape=(
            jax.ShapeDtypeStruct((4, 256, HEAD_DIM), jnp.bfloat16),
            jax.ShapeDtypeStruct((8, 256, HEAD_DIM), jnp.bfloat16),
        ),
        in_specs=[SMEM, VMEM, VMEM, VMEM],
        out_specs=(VMEM, VMEM),
        scratch_shapes=[
            pltpu.VMEM((1024, HEAD_DIM), jnp.int32),
            pltpu.VMEM((HEAD_DIM, 1024), jnp.float32),
        ],
        name="grads",
    )(span_place, stats_all, q_all, kv_all)

    dq_parts = lax.all_to_all(dq, Q_AXES, 0, 0, tiled=True)
    dq_rows = pl.pallas_call(
        dq_sum_kernel,
        out_shape=jax.ShapeDtypeStruct((256, HEAD_DIM), jnp.bfloat16),
        in_specs=[VMEM],
        out_specs=VMEM,
        name="dq_sum",
    )(dq_parts)
    dq_home = lax.all_to_all(dq_rows.reshape(32, 8, HEAD_DIM), HEADS_AXES, 0, 0, tiled=True)
    grad_query = dq_home.transpose(1, 0, 2).reshape(8, 32 * HEAD_DIM)

    dkv_parts = lax.all_to_all(dkv, KV_AXES, 0, 0, tiled=True)
    grad_key, grad_value = pl.pallas_call(
        dkv_sum_kernel,
        out_shape=(jax.ShapeDtypeStruct((128, 256), jnp.bfloat16),) * 2,
        in_specs=[VMEM],
        out_specs=(VMEM, VMEM),
        name="dkv_sum",
    )(dkv_parts)
    return grad_query, grad_key, grad_value


def solution(mesh):
    torus = Mesh(mesh.devices.reshape(4, 2, 2, 2, 8, 2), CTX_HEAD)
    return jax.shard_map(
        body,
        mesh=torus,
        in_specs=(
            P(CTX_HEAD, None),
            P(CTX, HEAD),
            P(CTX, HEAD),
            P(CTX_HEAD, None),
            P(CTX_HEAD, None),
            P(),
        ),
        out_specs=(P(CTX_HEAD, None), P(CTX, HEAD), P(CTX, HEAD)),
        check_vma=False,
    )
```

time: 376 us -> 131 us (0.35)
  waiting for transfers between devices: 226 us -> 24.1 us
  blocking collectives: 22.1 us -> 63.8 us
  local copies, waits for them, and re-layouts: 41.9 us -> 2.09 us
  other arithmetic: 28 us -> 1.62 us
  Pallas kernels: 0 us -> 16.2 us
  between operations: 14.2 us -> 0.65 us
  matrix products: 12 us -> 0 us
  starting transfers between devices: 30 us -> 21.9 us
    all_to_all x6 -> x3, waiting for transfers between devices: 210 us -> 24.1 us  [the longest x1 10.1 us: body(): own = lax.all_to_all(mine, HEADS_AXES, 0, 0, tiled=True)]
    all_to_all x1 -> x4, blocking collectives: 22.1 us -> 63.8 us  [the longest x1 20.2 us: body(): q_all = lax.all_to_all(q_send, Q_AXES, 0, 0, tiled=True)]
    dynamic_slice x24 -> x0, local copies, waits for them, and re-layouts: 18.4 us -> none  [body(): lax.scan(stat_scan, (start_top, start_total), (key_blocks, block_starts))]
    pallas_call x0 -> x6, Pallas kernels: none -> 16.2 us  [the longest x1 5.93 us: body(): pl.pallas_call(grads_kernel, out_shape=(jax.ShapeDtypeStruct((4, 256, HEA...]
    all_gather x1 -> x0, waiting for transfers between devices: 16.1 us -> none  [side_by_side(): lax.all_gather(both, axis, axis=dim, tiled=True)]
    dynamic_update_slice x12 -> x0, local copies, waits for them, and re-layouts: 13.4 us -> none  [body(): lax.scan(grad_scan, zeros_rows, (key_blocks, value_blocks, block_starts))]
    dot_general x24 -> x0, matrix products: 12 us -> none  [the longest x4 5.15 us: block_grads(): jnp.einsum('hrt,rhd->thd', dscores, query_heads, preferred_element_type=j...]
    concatenate x2 -> x0, other arithmetic: 9.1 us -> none  [the longest x1 7.57 us: sent_together(): both = jnp.concatenate(arrays, axis=along)]
  transfers between devices with their start and end apart: 7 -> 3, of which waited for: 7 -> 3; matrix products, arithmetic and copies ran while one was open for 3% -> 0% of each run, Pallas kernels for 0% -> 3%
where the time goes in v1:
time: 131 us; the launch traced here: 130 us
  blocking collectives  63.8 us (49%)
  waiting for transfers between devices  24.1 us (18%)
  starting transfers between devices  21.9 us (17%)
  Pallas kernels  16.2 us (12%)
  local copies, waits for them, and re-layouts  2.09 us (2%)
  other arithmetic  1.62 us (1%)
    all_to_all x1, blocking collectives, body(): q_all = lax.all_to_all(q_send, Q_AXES, 0, 0, tiled=True)  20.2 us
    all_to_all x1, blocking collectives, body(): lax.all_to_all(dq_rows.reshape(32, 8, HEAD_DIM), HEADS_AXES, 0, 0, tiled=...  19.1 us
    all_to_all x1, starting transfers between devices, body(): own = lax.all_to_all(mine, HEADS_AXES, 0, 0, tiled=True)  14.4 us
    all_to_all x1, blocking collectives, body(): dq_parts = lax.all_to_all(dq, Q_AXES, 0, 0, tiled=True)  13.1 us
    all_to_all x1, blocking collectives, body(): stats_all = lax.all_to_all(stats, Q_AXES, 0, 0, tiled=True)  11.4 us
    all_to_all x1, waiting for transfers between devices, body(): own = lax.all_to_all(mine, HEADS_AXES, 0, 0, tiled=True)  10.1 us
    all_to_all x1, waiting for transfers between devices, body(): dkv_parts = lax.all_to_all(dkv, KV_AXES, 0, 0, tiled=True)  7.92 us
    all_to_all x1, waiting for transfers between devices, body(): kv_all = lax.all_to_all(kv_send, KV_AXES, 0, 0, tiled=True)  6.09 us
  transfers between devices with their start and end apart: 3, of which 3 were waited for; matrix products, arithmetic and copies ran while one was open for 0% of the time, Pallas kernels for 3%

profile of v1, /device:TPU:1, one launch (start us, length us, event | category | flops | bytes accessed | tf_op | source)
XLA Modules:
  0.0 130.3 jit_solution(10117498849133456293)
XLA Ops:
  0.6 1.6 %pad_maximum_fusion = bf16[32,3,8,128]{3,2,1,0:T(8,128)(2,1)} fusion(bf16[32,1,8,128]{3,2,1,0:T(8,128)(2,1)} %bitcast.21, bf16[32,1,8,128]{3,2,1,0:T(8,128)(2,1)} %bitcast.22, bf16[32,1,8,128]{3,2,1,0:T(8,128)(2,1)} %bitcast.23), kind=kLoop, calls=%fused_computation | loop fusion | flops 196608 | bytes 393216 | tf_op jit(solution)/shard_map/stack | solution.py:148
  2.3 14.4 %all-to-all-start = ((bf16[32,3,8,128]{3,2,1,0:T(8,128)(2,1)}), bf16[32,3,8,128]{3,2,1,0:T(8,128)(2,1)S(1)}, u32[]{:S(2)}, u32[]{:S(2)}) async-start(bf16[32,3,8,128]{3,2,1,0:T(8,128)(2,1)} %pad_maximum_fusion), calls=%async_computation | async-start | bytes 393216 | tf_op jit(solution)/shard_map/all_to_all | solution.py:149
  16.7 1.7 %kv_pack.1 = bf16[8,256,128]{2,1,0:T(8,128)(2,1)} custom-call(bf16[128,256]{1,0:T(8,128)(2,1)} %key_ref.1, bf16[128,256]{1,0:T(8,128)(2,1)} %value_ref.1), custom_call_target="tpu_custom_call" | custom-call | tf_op jit(solution)/shard_map/kv_pack/pallas_call | solution.py:159
  18.4 10.1 %all-to-all-done.own_ref = bf16[32,3,8,128]{3,2,1,0:T(8,128)(2,1)S(1)} async-done(((bf16[32,3,8,128]{3,2,1,0:T(8,128)(2,1)}), bf16[32,3,8,128]{3,2,1,0:T(8,128)(2,1)S(1)}, u32[]{:S(2)}, u32[]{:S(2)}) %all-to-all-start) | async-done | bytes 196640 | tf_op jit(solution)/shard_map/all_to_all | solution.py:149
  28.5 0.0 copy-start.2
  28.5 0.7 copy-done.2
  29.2 3.6 %all-to-all-start.2 = ((bf16[8,256,128]{2,1,0:T(8,128)(2,1)}), bf16[8,256,128]{2,1,0:T(8,128)(2,1)S(1)}, u32[]{:S(2)}, u32[]{:S(2)}) async-start(bf16[8,256,128]{2,1,0:T(8,128)(2,1)} %kv_pack.1), calls=%async_computation.2 | async-start | bytes 1048576 | tf_op jit(solution)/shard_map/all_to_all | solution.py:166
  32.8 1.8 %q_pack.1 = bf16[4,32,2,8,128]{4,3,2,1,0:T(8,128)(2,1)} custom-call(bf16[32,3,8,128]{3,2,1,0:T(8,128)(2,1)} %copy-done.2), custom_call_target="tpu_custom_call" | custom-call | tf_op jit(solution)/shard_map/q_pack/pallas_call | solution.py:150
  34.6 6.1 %all-to-all-done.2.kv_ref = bf16[8,256,128]{2,1,0:T(8,128)(2,1)S(1)} async-done(((bf16[8,256,128]{2,1,0:T(8,128)(2,1)}), bf16[8,256,128]{2,1,0:T(8,128)(2,1)S(1)}, u32[]{:S(2)}, u32[]{:S(2)}) %all-to-all-start.2) | async-done | bytes 524320 | tf_op jit(solution)/shard_map/all_to_all | solution.py:166
  40.7 0.0 copy-start
  40.7 20.2 %all_to_all.35.q_ref = bf16[4,32,2,8,128]{4,3,2,1,0:T(8,128)(2,1)} all-to-all(bf16[4,32,2,8,128]{4,3,2,1,0:T(8,128)(2,1)} %q_pack.1), channel_id=1, replica_groups=mesh['yh'=4,'yl'=2,'xl'=2,'c'=2,'z'=8,'xh'=2] {'yh'}, dimensions={0} | all-to-all | bytes 1048576 | tf_op jit(solution)/shard_map/all_to_all | solution.py:157
  61.0 0.0 copy-done
  61.0 3.4 %stats.1 = f32[4,24,128]{2,1,0:T(8,128)} custom-call(s32[64]{0:T(128)} %place_ref.3, bf16[32,3,8,128]{3,2,1,0:T(8,128)(2,1)} %copy-done.2, bf16[4,32,2,8,128]{4,3,2,1,0:T(8,128)(2,1)} %all_to_all.35.q_ref, bf16[8,256,128]{2,1,0:T(8,128)(2,1)} %copy-done), custom_call_target="tpu_custom_call" | custom-call | tf_op jit(solution)/shard_map/stats/pallas_call | solution.py:168
  64.3 11.4 %all_to_all.36.stats_ref = f32[4,24,128]{2,1,0:T(8,128)} all-to-all(f32[4,24,128]{2,1,0:T(8,128)} %stats.1), channel_id=1, replica_groups=mesh['yh'=4,'yl'=2,'xl'=2,'c'=2,'z'=8,'xh'=2] {'yh'}, dimensions={0} | all-to-all | bytes 98304 | tf_op jit(solution)/shard_map/all_to_all | solution.py:176
  75.8 5.9 %grads.1 = (bf16[4,256,128]{2,1,0:T(8,128)(2,1)}, bf16[8,256,128]{2,1,0:T(8,128)(2,1)}) custom-call(s32[64]{0:T(128)} %place_ref.3, f32[4,24,128]{2,1,0:T(8,128)} %all_to_all.36.stats_ref, bf16[4,32,2,8,128]{4,3,2,1,0:T(8,128)(2,1)} %all_to_all.35.q_ref, bf16[8,256,128]{2,1,0:T(8,128)(2,1)} %copy-done), custom_call_target="tpu_custom_call" | custom-call | tf_op jit(solution)/shard_map/grads/pallas_call | solution.py:178
  81.7 13.1 %all_to_all.37.parts_ref = bf16[4,256,128]{2,1,0:T(8,128)(2,1)} all-to-all(bf16[4,256,128]{2,1,0:T(8,128)(2,1)} %get-tuple-element.7), channel_id=1, replica_groups=mesh['yh'=4,'yl'=2,'xl'=2,'c'=2,'z'=8,'xh'=2] {'yh'}, dimensions={0} | all-to-all | bytes 524288 | tf_op jit(solution)/shard_map/all_to_all | solution.py:193
  94.8 1.6 %dq_sum.1 = bf16[256,128]{1,0:T(8,128)(2,1)} custom-call(bf16[4,256,128]{2,1,0:T(8,128)(2,1)} %all_to_all.37.parts_ref), custom_call_target="tpu_custom_call" | custom-call | tf_op jit(solution)/shard_map/dq_sum/pallas_call | solution.py:194
  96.4 19.1 %all_to_all.38 = bf16[32,8,128]{2,1,0:T(8,128)(2,1)S(1)} all-to-all(bf16[32,8,128]{2,1,0:T(8,128)(2,1)} %bitcast.19), channel_id=1, replica_groups=mesh['yh'=4,'yl'=2,'xl'=2,'c'=2,'z'=8,'xh'=2] {'z','xh','c'}, dimensions={0} | all-to-all | bytes 131072 | tf_op jit(solution)/shard_map/all_to_all | solution.py:201
  115.4 3.8 %all-to-all-start.6 = ((bf16[8,256,128]{2,1,0:T(8,128)(2,1)}), bf16[8,256,128]{2,1,0:T(8,128)(2,1)S(1)}, u32[]{:S(2)}, u32[]{:S(2)}) async-start(bf16[8,256,128]{2,1,0:T(8,128)(2,1)} %get-tuple-element.8), calls=%async_computation.6 | async-start | bytes 1048576 | tf_op jit(solution)/shard_map/all_to_all | solution.py:204
  119.2 7.9 %all-to-all-done.6.parts_ref = bf16[8,256,128]{2,1,0:T(8,128)(2,1)S(1)} async-done(((bf16[8,256,128]{2,1,0:T(8,128)(2,1)}), bf16[8,256,128]{2,1,0:T(8,128)(2,1)S(1)}, u32[]{:S(2)}, u32[]{:S(2)}) %all-to-all-start.6) | async-done | bytes 524320 | tf_op jit(solution)/shard_map/all_to_all | solution.py:204
  127.1 0.0 copy-start.1
  127.2 0.8 copy-done.1
  127.9 1.7 %dkv_sum.1 = (bf16[128,256]{1,0:T(8,128)(2,1)}, bf16[128,256]{1,0:T(8,128)(2,1)}) custom-call(bf16[8,256,128]{2,1,0:T(8,128)(2,1)} %copy-done.1), custom_call_target="tpu_custom_call" | custom-call | tf_op jit(solution)/shard_map/dkv_sum/pallas_call | solution.py:205
  129.7 0.6 copy.10
Async XLA Ops:
  2.3 26.2 %all-to-all-start = ((bf16[32,3,8,128]{3,2,1,0:T(8,128)(2,1)}), bf16[32,3,8,128]{3,2,1,0:T(8,128)(2,1)S(1)}, u32[]{:S(2)}, u32[]{:S(2)}) async-start(bf16[32,3,8,128]{3,2,1,0:T(8,128)(2,1)} %pad_maximum_fusion), calls=%async_computation | async-start | bytes 393216 | tf_op jit(solution)/shard_map/all_to_all | solution.py:149
  28.5 0.7 copy-start.2
  29.2 11.6 %all-to-all-start.2 = ((bf16[8,256,128]{2,1,0:T(8,128)(2,1)}), bf16[8,256,128]{2,1,0:T(8,128)(2,1)S(1)}, u32[]{:S(2)}, u32[]{:S(2)}) async-start(bf16[8,256,128]{2,1,0:T(8,128)(2,1)} %kv_pack.1), calls=%async_computation.2 | async-start | bytes 1048576 | tf_op jit(solution)/shard_map/all_to_all | solution.py:166
  40.7 20.2 %copy-start = (bf16[8,256,128]{2,1,0:T(8,128)(2,1)}, bf16[8,256,128]{2,1,0:T(8,128)(2,1)S(1)}, u32[]{:S(2)}) copy-start(bf16[8,256,128]{2,1,0:T(8,128)(2,1)S(1)} %all-to-all-done.2.kv_ref) | copy-start | bytes 1572868
  115.4 11.7 %all-to-all-start.6 = ((bf16[8,256,128]{2,1,0:T(8,128)(2,1)}), bf16[8,256,128]{2,1,0:T(8,128)(2,1)S(1)}, u32[]{:S(2)}, u32[]{:S(2)}) async-start(bf16[8,256,128]{2,1,0:T(8,128)(2,1)} %get-tuple-element.8), calls=%async_computation.6 | async-start | bytes 1048576 | tf_op jit(solution)/shard_map/all_to_all | solution.py:204
  127.1 0.8 copy-start.1

commit v2 on v1

v2 whole, which is shorter than its diff:
```python
import jax
import jax.numpy as jnp
from jax import lax
from jax.experimental import pallas as pl
from jax.experimental.pallas import tpu as pltpu
from jax.sharding import Mesh
from jax.sharding import PartitionSpec as P


HEAD_DIM = 128
SCALE = HEAD_DIM ** (-0.5)
SPAN = 64
HEADS_AXES = ("z", "xh", "c")
Q_AXES = ("yl", "xl")
CTX_HEAD = ("yh", "yl", "xl", "c", "z", "xh")
CTX = ("yh", "yl", "xl", "c")
HEAD = ("z", "xh")
NEG = -1e30


def key_positions(place_ref, out_ref):
    row = lax.broadcasted_iota(jnp.int32, (SPAN, HEAD_DIM), 0)
    c = lax.axis_index("c")
    for p in range(4):
        back = lax.rem(lax.axis_index("yh") + (4 - p), 4)
        chip = (back * 2 + lax.axis_index("yl")) * 2 + lax.axis_index("xl")
        for q in range(2):
            first = chip * 4 + (c if q == 0 else 1 - c) * 2
            for k in range(2):
                at = ((p * 2 + q) * 2 + k) * SPAN
                out_ref[at : at + SPAN, :] = row + place_ref[first + k] * SPAN


def query_positions(place_ref, b):
    chip = lax.axis_index("yh") * 4 + b
    lane = lax.broadcasted_iota(jnp.int32, (1, 256), 1)
    core_one = ((lane // 8) % 2) == 1
    late = lane >= 128
    at = [[place_ref[chip * 4 + c * 2 + k] for k in range(2)] for c in range(2)]
    place = jnp.where(
        core_one,
        jnp.where(late, at[1][1], at[1][0]),
        jnp.where(late, at[0][1], at[0][0]),
    )
    return place * SPAN + ((lane // 16) % 8) * 8 + lane % 8


def rows_of(ref, b, k):
    return ref[b, :, k].astype(jnp.float32).reshape(256, HEAD_DIM).astype(jnp.bfloat16)


def dot(a, b, dims):
    return lax.dot_general(a, b, (dims, ((), ())), preferred_element_type=jnp.float32)


def stats_kernel(place_ref, own_ref, q_ref, kv0, kv1, kv2, kv3, out_ref, kpos_ref):
    key_positions(place_ref, kpos_ref)
    grad = own_ref[:, 1].astype(jnp.float32).reshape(256, HEAD_DIM)
    saved = own_ref[:, 2].astype(jnp.float32).reshape(256, HEAD_DIM)
    delta = jnp.sum((grad * saved).T, axis=0, keepdims=True)
    keys = jnp.concatenate(
        [kv[:, :128].reshape(256, HEAD_DIM) for kv in (kv0, kv1, kv2, kv3)], axis=0
    )
    kpos = jnp.concatenate([kpos_ref[...]] * 2, axis=1)
    zeros = jnp.zeros((6, HEAD_DIM), jnp.float32)
    tops, totals = [], []
    for b in range(4):
        scores = dot(keys, rows_of(q_ref, b, 0), ((1,), (1,))) * SCALE
        scores = jnp.where(kpos <= query_positions(place_ref, b), scores, -jnp.inf)
        top = jnp.maximum(jnp.max(scores, axis=0, keepdims=True), NEG)
        total = jnp.sum(jnp.exp(scores - top), axis=0, keepdims=True)
        for k in range(2):
            tops.append(top[:, k * 128 : (k + 1) * 128])
            totals.append(total[:, k * 128 : (k + 1) * 128])
    block = jnp.concatenate(
        tops + totals + [delta[:, :128], delta[:, 128:], zeros], axis=0
    )
    for p in range(4):
        out_ref[p] = block


def grads_kernel(
    place_ref, stats_ref, q_ref, kv0, kv1, kv2, kv3, dq_ref, d0, d1, d2, d3, kpos_ref, acc_ref
):
    key_positions(place_ref, kpos_ref)
    top = jnp.max(stats_ref[:, 0:8], axis=0)
    total = jnp.zeros((8, HEAD_DIM), jnp.float32)
    for p in range(4):
        total += stats_ref[p, 8:16] * jnp.exp(stats_ref[p, 0:8] - top)
    lse8 = top + jnp.log(total)
    lse = jnp.concatenate([lse8[j : j + 1] for j in range(8)], axis=1)
    delta = jnp.concatenate(
        [stats_ref[b, 16 + k : 17 + k] for b in range(4) for k in range(2)], axis=1
    )
    qpos = jnp.concatenate([query_positions(place_ref, b) for b in range(4)], axis=1)
    queries = jnp.concatenate([rows_of(q_ref, b, 0) for b in range(4)], axis=0)
    grads = jnp.concatenate([rows_of(q_ref, b, 1) for b in range(4)], axis=0)
    for j in range(8):
        kv_ref = (kv0, kv1, kv2, kv3)[j // 2]
        dkv_ref = (d0, d1, d2, d3)[j // 2]
        keys = kv_ref[j % 2, :128]
        values = kv_ref[j % 2, 128:]
        kpos = jnp.concatenate([kpos_ref[j * 128 : (j + 1) * 128, :]] * 8, axis=1)
        scores = dot(keys, queries, ((1,), (1,))) * SCALE
        probs = jnp.exp(jnp.where(kpos <= qpos, scores - lse, -jnp.inf))
        dprobs = dot(values, grads, ((1,), (1,)))
        dscores = (probs * (dprobs - delta) * SCALE).astype(jnp.bfloat16)
        dkv_ref[j % 2, :128] = dot(dscores, queries, ((1,), (0,))).astype(jnp.bfloat16)
        dkv_ref[j % 2, 128:] = dot(probs.astype(jnp.bfloat16), grads, ((1,), (0,))).astype(jnp.bfloat16)
        part = dot(keys.T, dscores, ((1,), (0,)))
        if j == 0:
            acc_ref[...] = part
        else:
            acc_ref[...] += part
    for b in range(4):
        dq_ref[b] = acc_ref[:, b * 256 : (b + 1) * 256].T.astype(jnp.bfloat16)


def half(ref, c):
    return ref[:, pl.ds(pl.multiple_of(c * HEAD_DIM, HEAD_DIM), HEAD_DIM)]


def kv_pack_kernel(key_ref, value_ref, keep_ref, give_ref):
    c = lax.axis_index("c")
    keep_ref[:128] = half(key_ref, c)
    keep_ref[128:] = half(value_ref, c)
    give_ref[:128] = half(key_ref, 1 - c)
    give_ref[128:] = half(value_ref, 1 - c)


def join_kernel(keep_ref, got_ref, out_ref):
    out_ref[0] = keep_ref[...]
    out_ref[1] = got_ref[...]


def q_pack_kernel(own_ref, out_ref):
    block = own_ref[:, :2]
    for p in range(4):
        out_ref[p] = block


def dq_sum_kernel(parts_ref, out_ref):
    total = parts_ref[0].astype(jnp.float32)
    for p in range(1, 4):
        total += parts_ref[p].astype(jnp.float32)
    out_ref[...] = total.astype(jnp.bfloat16)


def dkv_sum_kernel(p0, p1, p2, p3, keep_ref, give_ref):
    for q, out_ref in enumerate((keep_ref, give_ref)):
        total = p0[q].astype(jnp.float32)
        for part in (p1, p2, p3):
            total += part[q].astype(jnp.float32)
        out_ref[...] = total.astype(jnp.bfloat16)


def dkv_place_kernel(keep_ref, got_ref, dk_ref, dv_ref):
    c = lax.axis_index("c")
    for ref, at in ((keep_ref, c), (got_ref, 1 - c)):
        columns = pl.ds(pl.multiple_of(at * HEAD_DIM, HEAD_DIM), HEAD_DIM)
        dk_ref[:, columns] = ref[:128]
        dv_ref[:, columns] = ref[128:]


VMEM = pl.BlockSpec(memory_space=pltpu.VMEM)
SMEM = pl.BlockSpec(memory_space=pltpu.SMEM)


def kernel_call(kernel, *, out_shape, in_specs, **options):
    shapes = [pltpu.VMEM(s.shape, s.dtype) for s in jax.tree.leaves(out_shape)]
    call = pl.pallas_call(
        kernel,
        in_specs=in_specs,
        out_shape=shapes[0] if len(shapes) == 1 else tuple(shapes),
        compiler_params=pltpu.CompilerParams(vmem_limit_bytes=32 * 1024 * 1024),
        **options,
    )

    def run(*arrays):
        placed = [
            pltpu.with_memory_space_constraint(a, pltpu.VMEM) if spec is VMEM else a
            for a, spec in zip(arrays, in_specs)
        ]
        return call(*placed)

    return run


def head_tiles(x):
    return x.reshape(8, 32, HEAD_DIM).transpose(1, 0, 2)


def exchange(x, axes):
    return lax.all_to_all(x, axes, 0, 0, tiled=True)


def shift(x, axis, by):
    n = lax.axis_size(axis)
    return lax.ppermute(x, axis, [(i, (i + by) % n) for i in range(n)])


def bf16(*shape):
    return jax.ShapeDtypeStruct(shape, jnp.bfloat16)


def body(query_in, key_in, value_in, out_saved, out_grad, span_place):
    keep, give = kernel_call(
        kv_pack_kernel,
        out_shape=(bf16(256, HEAD_DIM),) * 2,
        in_specs=[VMEM, VMEM],
        out_specs=(VMEM, VMEM),
    )(key_in, value_in)
    got = shift(give, "c", 1)
    kv = kernel_call(
        join_kernel,
        out_shape=bf16(2, 256, HEAD_DIM),
        in_specs=[VMEM, VMEM],
        out_specs=VMEM,
    )(keep, got)
    kvs = [kv] + [shift(kv, "yh", k) for k in (1, 2, 3)]

    mine = jnp.stack([head_tiles(query_in), head_tiles(out_grad), head_tiles(out_saved)], axis=1)
    own = exchange(mine, HEADS_AXES)
    q_send = kernel_call(
        q_pack_kernel,
        out_shape=bf16(4, 32, 2, 8, HEAD_DIM),
        in_specs=[VMEM],
        out_specs=VMEM,
    )(own)
    q_all = exchange(q_send, Q_AXES)

    stats = kernel_call(
        stats_kernel,
        out_shape=jax.ShapeDtypeStruct((4, 24, HEAD_DIM), jnp.float32),
        in_specs=[SMEM] + [VMEM] * 6,
        out_specs=VMEM,
        scratch_shapes=[pltpu.VMEM((1024, HEAD_DIM), jnp.int32)],
    )(span_place, own, q_all, *kvs)
    stats_all = exchange(stats, Q_AXES)

    dq, *dkvs = kernel_call(
        grads_kernel,
        out_shape=(bf16(4, 256, HEAD_DIM),) + (bf16(2, 256, HEAD_DIM),) * 4,
        in_specs=[SMEM] + [VMEM] * 6,
        out_specs=(VMEM,) * 5,
        scratch_shapes=[
            pltpu.VMEM((1024, HEAD_DIM), jnp.int32),
            pltpu.VMEM((HEAD_DIM, 1024), jnp.float32),
        ],
    )(span_place, stats_all, q_all, *kvs)

    parts = [dkvs[0]] + [shift(dkvs[k], "yh", -k) for k in (1, 2, 3)]
    dq_parts = exchange(dq, Q_AXES)
    dq_rows = kernel_call(
        dq_sum_kernel, out_shape=bf16(256, HEAD_DIM), in_specs=[VMEM], out_specs=VMEM
    )(dq_parts)
    dq_home = exchange(dq_rows.reshape(32, 8, HEAD_DIM), HEADS_AXES)
    grad_query = dq_home.transpose(1, 0, 2).reshape(8, 32 * HEAD_DIM)

    keep, give = kernel_call(
        dkv_sum_kernel,
        out_shape=(bf16(256, HEAD_DIM),) * 2,
        in_specs=[VMEM] * 4,
        out_specs=(VMEM, VMEM),
    )(*parts)
    got = shift(give, "c", 1)
    grad_key, grad_value = kernel_call(
        dkv_place_kernel,
        out_shape=(bf16(128, 256),) * 2,
        in_specs=[VMEM, VMEM],
        out_specs=(VMEM, VMEM),
    )(keep, got)
    return grad_query, grad_key, grad_value


def solution(mesh):
    torus = Mesh(mesh.devices.reshape(4, 2, 2, 2, 8, 2), CTX_HEAD)
    return jax.shard_map(
        body,
        mesh=torus,
        in_specs=(
            P(CTX_HEAD, None),
            P(CTX, HEAD),
            P(CTX, HEAD),
            P(CTX_HEAD, None),
            P(CTX_HEAD, None),
            P(),
        ),
        out_specs=(P(CTX_HEAD, None), P(CTX, HEAD), P(CTX, HEAD)),
        check_vma=False,
    )
```

time: 131 us -> 107 us (0.82)
  blocking collectives: 63.8 us -> 37.2 us
  starting transfers between devices: 21.9 us -> 44.9 us
  waiting for transfers between devices: 24.1 us -> 11.3 us
  Pallas kernels: 16.2 us -> 8.82 us
    ppermute x0 -> x8, starting transfers between devices: none -> 31.6 us  [shift(): return lax.ppermute(x, axis, [(i, (i + by) % n) for i in range(n)])]
    all_to_all x4 -> x2, blocking collectives: 63.8 us -> 37.2 us  [exchange(): return lax.all_to_all(x, axes, 0, 0, tiled=True)]
    all_to_all x3, waiting for transfers between devices: 24.1 us -> 4.28 us  [exchange(): return lax.all_to_all(x, axes, 0, 0, tiled=True)]
    all_to_all x3, starting transfers between devices: 21.9 us -> 13.4 us  [exchange(): return lax.all_to_all(x, axes, 0, 0, tiled=True)]
    pallas_call x6 -> x8, Pallas kernels: 16.2 us -> 8.82 us  [run(): return call(*placed)]
    ppermute x0 -> x8, waiting for transfers between devices: none -> 7.07 us  [shift(): return lax.ppermute(x, axis, [(i, (i + by) % n) for i in range(n)])]
  transfers between devices with their start and end apart: 3 -> 11, of which waited for: 3 -> 4; matrix products, arithmetic and copies ran while one was open for 0% -> 1% of each run, Pallas kernels for 3% -> 1%
where the time goes in v2:
time: 107 us; the launch traced here: 106 us
  starting transfers between devices  44.9 us (42%)
  blocking collectives  37.2 us (35%)
  waiting for transfers between devices  11.3 us (11%)
  Pallas kernels  8.82 us (8%)
  local copies, waits for them, and re-layouts  1.9 us (2%)
    all_to_all x2, blocking collectives, exchange(): return lax.all_to_all(x, axes, 0, 0, tiled=True)  37.2 us
    ppermute x8, starting transfers between devices, shift(): return lax.ppermute(x, axis, [(i, (i + by) % n) for i in range(n)])  31.6 us
    all_to_all x3, starting transfers between devices, exchange(): return lax.all_to_all(x, axes, 0, 0, tiled=True)  13.4 us
    pallas_call x8, Pallas kernels, run(): return call(*placed)  8.82 us
    ppermute x8, waiting for transfers between devices, shift(): return lax.ppermute(x, axis, [(i, (i + by) % n) for i in range(n)])  7.07 us
    all_to_all x3, waiting for transfers between devices, exchange(): return lax.all_to_all(x, axes, 0, 0, tiled=True)  4.28 us
  transfers between devices with their start and end apart: 11, of which 4 were waited for; matrix products, arithmetic and copies ran while one was open for 1% of the time, Pallas kernels for 1%

profile of v2, /device:TPU:1, one launch (start us, length us, event | category | flops | bytes accessed | tf_op | source)
XLA Modules:
  0.0 105.9 jit_solution(1075294200679058465)
XLA Ops:
  0.6 0.9 pad_maximum_fusion
  1.6 26.0 %all_to_all.25.own_ref = bf16[32,3,8,128]{3,2,1,0:T(8,128)(2,1)S(1)} all-to-all(bf16[32,3,8,128]{3,2,1,0:T(8,128)(2,1)S(1)} %pad_maximum_fusion), channel_id=1, replica_groups=mesh['yh'=4,'yl'=2,'xl'=2,'c'=2,'z'=8,'xh'=2] {'z','xh','c'}, dimensions={0} | all-to-all | bytes 393216 | tf_op jit(solution)/shard_map/all_to_all | solution.py:194
  27.6 0.9 shard_map.85
  28.5 3.6 %all-to-all-start.1 = ((bf16[4,32,2,8,128]{4,3,2,1,0:T(8,128)(2,1)}), bf16[4,32,2,8,128]{4,3,2,1,0:T(8,128)(2,1)S(1)}, u32[]{:S(2)}, u32[]{:S(2)}) async-start(bf16[4,32,2,8,128]{4,3,2,1,0:T(8,128)(2,1)} %shard_map.85), calls=%async_computation.1 | async-start | bytes 1048576 | tf_op jit(solution)/shard_map/all_to_all | solution.py:194
  32.2 2.2 %collective-permute-start = (bf16[256,128]{1,0:T(8,128)(2,1)S(1)}, bf16[256,128]{1,0:T(8,128)(2,1)S(1)}, u32[]{:S(2)}, u32[]{:S(2)}) collective-permute-start(bf16[256,128]{1,0:T(8,128)(2,1)S(1)} %get-tuple-element.15), channel_id=1, source_target_pairs={{0,16},{16,0},{1,17},{17,1},{2,18},{18,2},{3,19},{19,3},{4,20},{20... | collective-permute-start | bytes 196616 | tf_op jit(solution)/shard_map/ppermute | solution.py:199
  34.3 1.0 collective-permute-done.got_ref
  35.3 5.9 %collective-permute-start.3 = (bf16[2,256,128]{2,1,0:T(8,128)(2,1)S(1)}, bf16[2,256,128]{2,1,0:T(8,128)(2,1)S(1)}, u32[]{:S(2)}, u32[]{:S(2)}) collective-permute-start(bf16[2,256,128]{2,1,0:T(8,128)(2,1)S(1)} %shard_map.87.kv0), channel_id=1, source_target_pairs={{0,384},{128,0},{256,128},{384,256},{1,385},{129,1},{257,129},{385... | collective-permute-start | bytes 393224 | tf_op jit(solution)/shard_map/ppermute | solution.py:199
  41.2 3.5 %collective-permute-start.2 = (bf16[2,256,128]{2,1,0:T(8,128)(2,1)S(1)}, bf16[2,256,128]{2,1,0:T(8,128)(2,1)S(1)}, u32[]{:S(2)}, u32[]{:S(2)}) collective-permute-start(bf16[2,256,128]{2,1,0:T(8,128)(2,1)S(1)} %shard_map.87.kv0), channel_id=1, source_target_pairs={{0,256},{128,384},{256,0},{384,128},{1,257},{129,385},{257,1},{385... | collective-permute-start | bytes 393224 | tf_op jit(solution)/shard_map/ppermute | solution.py:199
  44.7 4.2 %collective-permute-start.1 = (bf16[2,256,128]{2,1,0:T(8,128)(2,1)S(1)}, bf16[2,256,128]{2,1,0:T(8,128)(2,1)S(1)}, u32[]{:S(2)}, u32[]{:S(2)}) collective-permute-start(bf16[2,256,128]{2,1,0:T(8,128)(2,1)S(1)} %shard_map.87.kv0), channel_id=1, source_target_pairs={{0,128},{128,256},{256,384},{384,0},{1,129},{129,257},{257,385},{3... | collective-permute-start | bytes 393224 | tf_op jit(solution)/shard_map/ppermute | solution.py:199
  49.0 5.2 %collective-permute-done.2.kv2 = bf16[2,256,128]{2,1,0:T(8,128)(2,1)S(1)} collective-permute-done((bf16[2,256,128]{2,1,0:T(8,128)(2,1)S(1)}, bf16[2,256,128]{2,1,0:T(8,128)(2,1)S(1)}, u32[]{:S(2)}, u32[]{:S(2)}) %collective-permute-start.2) | collective-permute-done | bytes 131104 | tf_op jit(solution)/shard_map/ppermute | solution.py:199
  54.2 2.0 %shard_map.88 = f32[4,24,128]{2,1,0:T(8,128)S(1)} custom-call(s32[64]{0:T(128)S(1)} %copy-done.2, bf16[32,3,8,128]{3,2,1,0:T(8,128)(2,1)S(1)} %all_to_all.25.own_ref, bf16[4,32,2,8,128]{4,3,2,1,0:T(8,128)(2,1)S(1)} %all-to-all-done.1.q_ref, bf16[2,256,128]{2,1,0:T(8,128)(2,1)S(1)} %shard_map.87.kv0, bf16[2,256,128]{2,1,0:T(8,128)(2,1)S(1)} %collective-permute-done.1.kv1, ...), custom_call_target="tpu_custom_call" | custom-call | tf_op jit(solution)/shard_map/pallas_call | solution.py:184
  56.2 11.1 %all_to_all.26.stats_ref = f32[4,24,128]{2,1,0:T(8,128)S(1)} all-to-all(f32[4,24,128]{2,1,0:T(8,128)S(1)} %shard_map.88), channel_id=1, replica_groups=mesh['yh'=4,'yl'=2,'xl'=2,'c'=2,'z'=8,'xh'=2] {'yl','xl'}, dimensions={0} | all-to-all | bytes 98304 | tf_op jit(solution)/shard_map/all_to_all | solution.py:194
  67.3 5.1 %shard_map.89 = (bf16[4,256,128]{2,1,0:T(8,128)(2,1)}, bf16[2,256,128]{2,1,0:T(8,128)(2,1)S(1)}, bf16[2,256,128]{2,1,0:T(8,128)(2,1)S(1)}, bf16[2,256,128]{2,1,0:T(8,128)(2,1)S(1)}, bf16[2,256,128]{2,1,0:T(8,128)(2,1)S(1)}) custom-call(s32[64]{0:T(128)S(1)} %copy-done.2, f32[4,24,128]{2,1,0:T(8,128)S(1)} %all_to_all.26.stats_ref, ...), custom_call_target="tpu_custom_call" | custom-call | tf_op jit(solution)/shard_map/pallas_call | solution.py:184
  72.5 3.4 %all-to-all-start.3 = ((bf16[4,256,128]{2,1,0:T(8,128)(2,1)}), bf16[4,256,128]{2,1,0:T(8,128)(2,1)S(1)}, u32[]{:S(2)}, u32[]{:S(2)}) async-start(bf16[4,256,128]{2,1,0:T(8,128)(2,1)} %get-tuple-element.16), calls=%async_computation.3 | async-start | bytes 524288 | tf_op jit(solution)/shard_map/all_to_all | solution.py:194
  75.9 4.9 %collective-permute-start.4 = (bf16[2,256,128]{2,1,0:T(8,128)(2,1)S(1)}, bf16[2,256,128]{2,1,0:T(8,128)(2,1)S(1)}, u32[]{:S(2)}, u32[]{:S(2)}) collective-permute-start(bf16[2,256,128]{2,1,0:T(8,128)(2,1)S(1)} %get-tuple-element.18), channel_id=1, source_target_pairs={{0,384},{128,0},{256,128},{384,256},{1,385},{129,1},{257,129},{385... | collective-permute-start | bytes 393224 | tf_op jit(solution)/shard_map/ppermute | solution.py:199
  80.8 3.6 %collective-permute-start.5 = (bf16[2,256,128]{2,1,0:T(8,128)(2,1)S(1)}, bf16[2,256,128]{2,1,0:T(8,128)(2,1)S(1)}, u32[]{:S(2)}, u32[]{:S(2)}) collective-permute-start(bf16[2,256,128]{2,1,0:T(8,128)(2,1)S(1)} %get-tuple-element.19), channel_id=1, source_target_pairs={{0,256},{128,384},{256,0},{384,128},{1,257},{129,385},{257,1},{385... | collective-permute-start | bytes 393224 | tf_op jit(solution)/shard_map/ppermute | solution.py:199
  84.4 4.0 %collective-permute-start.6 = (bf16[2,256,128]{2,1,0:T(8,128)(2,1)S(1)}, bf16[2,256,128]{2,1,0:T(8,128)(2,1)S(1)}, u32[]{:S(2)}, u32[]{:S(2)}) collective-permute-start(bf16[2,256,128]{2,1,0:T(8,128)(2,1)S(1)} %get-tuple-element.20), channel_id=1, source_target_pairs={{0,128},{128,256},{256,384},{384,0},{1,129},{129,257},{257,385},{3... | collective-permute-start | bytes 393224 | tf_op jit(solution)/shard_map/ppermute | solution.py:199
  88.5 0.7 shard_map.90
  89.1 6.3 %all-to-all-start.4 = ((bf16[32,8,128]{2,1,0:T(8,128)(2,1)}), bf16[32,8,128]{2,1,0:T(8,128)(2,1)S(1)}, u32[]{:S(2)}, u32[]{:S(2)}) async-start(bf16[32,8,128]{2,1,0:T(8,128)(2,1)} %bitcast.9), calls=%async_computation.4 | async-start | bytes 131072 | tf_op jit(solution)/shard_map/all_to_all | solution.py:194
  95.6 3.2 %collective-permute-start.7 = (bf16[256,128]{1,0:T(8,128)(2,1)S(1)}, bf16[256,128]{1,0:T(8,128)(2,1)S(1)}, u32[]{:S(2)}, u32[]{:S(2)}) collective-permute-start(bf16[256,128]{1,0:T(8,128)(2,1)S(1)} %get-tuple-element.22), channel_id=1, source_target_pairs={{0,16},{16,0},{1,17},{17,1},{2,18},{18,2},{3,19},{19,3},{4,20},{20... | collective-permute-start | bytes 196616 | tf_op jit(solution)/shard_map/ppermute | solution.py:199
  98.8 0.9 collective-permute-done.7.got_ref
  99.7 0.6 copy.10
  101.0 4.3 %all-to-all-done.4 = bf16[32,8,128]{2,1,0:T(8,128)(2,1)S(1)} async-done(((bf16[32,8,128]{2,1,0:T(8,128)(2,1)}), bf16[32,8,128]{2,1,0:T(8,128)(2,1)S(1)}, u32[]{:S(2)}, u32[]{:S(2)}) %all-to-all-start.4) | async-done | bytes 65568 | tf_op jit(solution)/shard_map/all_to_all | solution.py:194
  105.3 0.6 copy.12
  (18 shorter events, 0.8 us)
Async XLA Ops:
  28.5 3.6 %copy-start = (bf16[128,256]{1,0:T(8,128)(2,1)S(1)}, bf16[128,256]{1,0:T(8,128)(2,1)}, u32[]{:S(2)}) copy-start(bf16[128,256]{1,0:T(8,128)(2,1)} %key_ref.1) | copy-start | bytes 196612
  28.5 3.6 %copy-start.1 = (bf16[128,256]{1,0:T(8,128)(2,1)S(1)}, bf16[128,256]{1,0:T(8,128)(2,1)}, u32[]{:S(2)}) copy-start(bf16[128,256]{1,0:T(8,128)(2,1)} %value_ref.1) | copy-start | bytes 196612
  28.5 25.7 %all-to-all-start.1 = ((bf16[4,32,2,8,128]{4,3,2,1,0:T(8,128)(2,1)}), bf16[4,32,2,8,128]{4,3,2,1,0:T(8,128)(2,1)S(1)}, u32[]{:S(2)}, u32[]{:S(2)}) async-start(bf16[4,32,2,8,128]{4,3,2,1,0:T(8,128)(2,1)} %shard_map.85), calls=%async_computation.1 | async-start | bytes 1048576 | tf_op jit(solution)/shard_map/all_to_all | solution.py:194
  32.2 3.1 %collective-permute-start = (bf16[256,128]{1,0:T(8,128)(2,1)S(1)}, bf16[256,128]{1,0:T(8,128)(2,1)S(1)}, u32[]{:S(2)}, u32[]{:S(2)}) collective-permute-start(bf16[256,128]{1,0:T(8,128)(2,1)S(1)} %get-tuple-element.15), channel_id=1, source_target_pairs={{0,16},{16,0},{1,17},{17,1},{2,18},{18,2},{3,19},{19,3},{4,20},{20... | collective-permute-start | bytes 196616 | tf_op jit(solution)/shard_map/ppermute | solution.py:199
  35.3 18.9 %copy-start.2 = (s32[64]{0:T(128)S(1)}, s32[64]{0:T(128)}, u32[]{:S(2)}) copy-start(s32[64]{0:T(128)} %place_ref.3) | copy-start | bytes 772
  35.3 13.7 %collective-permute-start.3 = (bf16[2,256,128]{2,1,0:T(8,128)(2,1)S(1)}, bf16[2,256,128]{2,1,0:T(8,128)(2,1)S(1)}, u32[]{:S(2)}, u32[]{:S(2)}) collective-permute-start(bf16[2,256,128]{2,1,0:T(8,128)(2,1)S(1)} %shard_map.87.kv0), channel_id=1, source_target_pairs={{0,384},{128,0},{256,128},{384,256},{1,385},{129,1},{257,129},{385... | collective-permute-start | bytes 393224 | tf_op jit(solution)/shard_map/ppermute | solution.py:199
  41.2 13.0 %collective-permute-start.2 = (bf16[2,256,128]{2,1,0:T(8,128)(2,1)S(1)}, bf16[2,256,128]{2,1,0:T(8,128)(2,1)S(1)}, u32[]{:S(2)}, u32[]{:S(2)}) collective-permute-start(bf16[2,256,128]{2,1,0:T(8,128)(2,1)S(1)} %shard_map.87.kv0), channel_id=1, source_target_pairs={{0,256},{128,384},{256,0},{384,128},{1,257},{129,385},{257,1},{385... | collective-permute-start | bytes 393224 | tf_op jit(solution)/shard_map/ppermute | solution.py:199
  44.7 9.4 %collective-permute-start.1 = (bf16[2,256,128]{2,1,0:T(8,128)(2,1)S(1)}, bf16[2,256,128]{2,1,0:T(8,128)(2,1)S(1)}, u32[]{:S(2)}, u32[]{:S(2)}) collective-permute-start(bf16[2,256,128]{2,1,0:T(8,128)(2,1)S(1)} %shard_map.87.kv0), channel_id=1, source_target_pairs={{0,128},{128,256},{256,384},{384,0},{1,129},{129,257},{257,385},{3... | collective-permute-start | bytes 393224 | tf_op jit(solution)/shard_map/ppermute | solution.py:199
  72.5 16.0 %all-to-all-start.3 = ((bf16[4,256,128]{2,1,0:T(8,128)(2,1)}), bf16[4,256,128]{2,1,0:T(8,128)(2,1)S(1)}, u32[]{:S(2)}, u32[]{:S(2)}) async-start(bf16[4,256,128]{2,1,0:T(8,128)(2,1)} %get-tuple-element.16), calls=%async_computation.3 | async-start | bytes 524288 | tf_op jit(solution)/shard_map/all_to_all | solution.py:194
  75.9 19.6 %collective-permute-start.4 = (bf16[2,256,128]{2,1,0:T(8,128)(2,1)S(1)}, bf16[2,256,128]{2,1,0:T(8,128)(2,1)S(1)}, u32[]{:S(2)}, u32[]{:S(2)}) collective-permute-start(bf16[2,256,128]{2,1,0:T(8,128)(2,1)S(1)} %get-tuple-element.18), channel_id=1, source_target_pairs={{0,384},{128,0},{256,128},{384,256},{1,385},{129,1},{257,129},{385... | collective-permute-start | bytes 393224 | tf_op jit(solution)/shard_map/ppermute | solution.py:199
  80.8 14.7 %collective-permute-start.5 = (bf16[2,256,128]{2,1,0:T(8,128)(2,1)S(1)}, bf16[2,256,128]{2,1,0:T(8,128)(2,1)S(1)}, u32[]{:S(2)}, u32[]{:S(2)}) collective-permute-start(bf16[2,256,128]{2,1,0:T(8,128)(2,1)S(1)} %get-tuple-element.19), channel_id=1, source_target_pairs={{0,256},{128,384},{256,0},{384,128},{1,257},{129,385},{257,1},{385... | collective-permute-start | bytes 393224 | tf_op jit(solution)/shard_map/ppermute | solution.py:199
  84.4 11.1 %collective-permute-start.6 = (bf16[2,256,128]{2,1,0:T(8,128)(2,1)S(1)}, bf16[2,256,128]{2,1,0:T(8,128)(2,1)S(1)}, u32[]{:S(2)}, u32[]{:S(2)}) collective-permute-start(bf16[2,256,128]{2,1,0:T(8,128)(2,1)S(1)} %get-tuple-element.20), channel_id=1, source_target_pairs={{0,128},{128,256},{256,384},{384,0},{1,129},{129,257},{257,385},{3... | collective-permute-start | bytes 393224 | tf_op jit(solution)/shard_map/ppermute | solution.py:199
  89.1 16.1 %all-to-all-start.4 = ((bf16[32,8,128]{2,1,0:T(8,128)(2,1)}), bf16[32,8,128]{2,1,0:T(8,128)(2,1)S(1)}, u32[]{:S(2)}, u32[]{:S(2)}) async-start(bf16[32,8,128]{2,1,0:T(8,128)(2,1)} %bitcast.9), calls=%async_computation.4 | async-start | bytes 131072 | tf_op jit(solution)/shard_map/all_to_all | solution.py:194
  95.6 4.1 %collective-permute-start.7 = (bf16[256,128]{1,0:T(8,128)(2,1)S(1)}, bf16[256,128]{1,0:T(8,128)(2,1)S(1)}, u32[]{:S(2)}, u32[]{:S(2)}) collective-permute-start(bf16[256,128]{1,0:T(8,128)(2,1)S(1)} %get-tuple-element.22), channel_id=1, source_target_pairs={{0,16},{16,0},{1,17},{17,1},{2,18},{18,2},{3,19},{19,3},{4,20},{20... | collective-permute-start | bytes 196616 | tf_op jit(solution)/shard_map/ppermute | solution.py:199

commit v3 on v2

--- a/solution.py
+++ b/solution.py
@@ -79,6 +79,11 @@
         out_ref[p] = block
 
 
+def block_rows(kv_refs, first, count, k):
+    at = slice(k * 128, (k + 1) * 128)
+    return jnp.concatenate([kv_refs[j // 2][j % 2, at] for j in range(first, first + count)], axis=0)
+
+
 def grads_kernel(
     place_ref, stats_ref, q_ref, kv0, kv1, kv2, kv3, dq_ref, d0, d1, d2, d3, kpos_ref, acc_ref
 ):
@@ -95,20 +100,24 @@
     qpos = jnp.concatenate([query_positions(place_ref, b) for b in range(4)], axis=1)
     queries = jnp.concatenate([rows_of(q_ref, b, 0) for b in range(4)], axis=0)
     grads = jnp.concatenate([rows_of(q_ref, b, 1) for b in range(4)], axis=0)
-    for j in range(8):
-        kv_ref = (kv0, kv1, kv2, kv3)[j // 2]
-        dkv_ref = (d0, d1, d2, d3)[j // 2]
-        keys = kv_ref[j % 2, :128]
-        values = kv_ref[j % 2, 128:]
-        kpos = jnp.concatenate([kpos_ref[j * 128 : (j + 1) * 128, :]] * 8, axis=1)
+    step = 4
+    for first in range(0, 8, step):
+        keys = block_rows((kv0, kv1, kv2, kv3), first, step, 0)
+        values = block_rows((kv0, kv1, kv2, kv3), first, step, 1)
+        kpos = kpos_ref[first * 128 : (first + step) * 128, :]
+        kpos = jnp.concatenate([kpos] * 8, axis=1)
         scores = dot(keys, queries, ((1,), (1,))) * SCALE
         probs = jnp.exp(jnp.where(kpos <= qpos, scores - lse, -jnp.inf))
         dprobs = dot(values, grads, ((1,), (1,)))
         dscores = (probs * (dprobs - delta) * SCALE).astype(jnp.bfloat16)
-        dkv_ref[j % 2, :128] = dot(dscores, queries, ((1,), (0,))).astype(jnp.bfloat16)
-        dkv_ref[j % 2, 128:] = dot(probs.astype(jnp.bfloat16), grads, ((1,), (0,))).astype(jnp.bfloat16)
+        dk = dot(dscores, queries, ((1,), (0,))).astype(jnp.bfloat16)
+        dv = dot(probs.astype(jnp.bfloat16), grads, ((1,), (0,))).astype(jnp.bfloat16)
+        for i in range(step):
+            d_ref = (d0, d1, d2, d3)[(first + i) // 2]
+            d_ref[i % 2, :128] = dk[i * 128 : (i + 1) * 128]
+            d_ref[i % 2, 128:] = dv[i * 128 : (i + 1) * 128]
         part = dot(keys.T, dscores, ((1,), (0,)))
-        if j == 0:
+        if first == 0:
             acc_ref[...] = part
         else:
             acc_ref[...] += part
@@ -166,12 +175,12 @@
 SMEM = pl.BlockSpec(memory_space=pltpu.SMEM)
 
 
-def kernel_call(kernel, *, out_shape, in_specs, **options):
+def kernel_call(kernel, *, out_shape, in_specs, final=False, **options):
     shapes = [pltpu.VMEM(s.shape, s.dtype) for s in jax.tree.leaves(out_shape)]
     call = pl.pallas_call(
         kernel,
         in_specs=in_specs,
-        out_shape=shapes[0] if len(shapes) == 1 else tuple(shapes),
+        out_shape=out_shape if final else shapes[0] if len(shapes) == 1 else tuple(shapes),
         compiler_params=pltpu.CompilerParams(vmem_limit_bytes=32 * 1024 * 1024),
         **options,
     )
@@ -212,20 +221,14 @@
     )(key_in, value_in)
     got = shift(give, "c", 1)
     kv = kernel_call(
-        join_kernel,
-        out_shape=bf16(2, 256, HEAD_DIM),
-        in_specs=[VMEM, VMEM],
-        out_specs=VMEM,
+        join_kernel, out_shape=bf16(2, 256, HEAD_DIM), in_specs=[VMEM, VMEM], out_specs=VMEM
     )(keep, got)
     kvs = [kv] + [shift(kv, "yh", k) for k in (1, 2, 3)]
 
     mine = jnp.stack([head_tiles(query_in), head_tiles(out_grad), head_tiles(out_saved)], axis=1)
     own = exchange(mine, HEADS_AXES)
     q_send = kernel_call(
-        q_pack_kernel,
-        out_shape=bf16(4, 32, 2, 8, HEAD_DIM),
-        in_specs=[VMEM],
-        out_specs=VMEM,
+        q_pack_kernel, out_shape=bf16(4, 32, 2, 8, HEAD_DIM), in_specs=[VMEM], out_specs=VMEM
     )(own)
     q_all = exchange(q_send, Q_AXES)
 
@@ -269,6 +272,7 @@
         out_shape=(bf16(128, 256),) * 2,
         in_specs=[VMEM, VMEM],
         out_specs=(VMEM, VMEM),
+        final=True,
     )(keep, got)
     return grad_query, grad_key, grad_value
 

time: 107 us -> 106 us (level)
  local copies, waits for them, and re-layouts: 1.9 us -> 0.64 us
    unnamed x9 -> x7, local copies, waits for them, and re-layouts: 1.9 us -> 0.64 us
  transfers between devices with their start and end apart: 11 -> 11, of which waited for: 4 -> 4; matrix products, arithmetic and copies ran while one was open for 1% -> 0% of each run, Pallas kernels for 1% -> 1%
where the time goes in v3:
time: 106 us; the launch traced here: 105 us
  starting transfers between devices  44.9 us (42%)
  blocking collectives  37.2 us (35%)
  waiting for transfers between devices  12 us (11%)
  Pallas kernels  8.54 us (8%)
    all_to_all x2, blocking collectives, exchange(): return lax.all_to_all(x, axes, 0, 0, tiled=True)  37.2 us
    ppermute x8, starting transfers between devices, shift(): return lax.ppermute(x, axis, [(i, (i + by) % n) for i in range(n)])  31.6 us
    all_to_all x3, starting transfers between devices, exchange(): return lax.all_to_all(x, axes, 0, 0, tiled=True)  13.3 us
    pallas_call x8, Pallas kernels, run(): return call(*placed)  8.54 us
    ppermute x8, waiting for transfers between devices, shift(): return lax.ppermute(x, axis, [(i, (i + by) % n) for i in range(n)])  7.07 us
    all_to_all x3, waiting for transfers between devices, exchange(): return lax.all_to_all(x, axes, 0, 0, tiled=True)  4.89 us
  transfers between devices with their start and end apart: 11, of which 4 were waited for; matrix products, arithmetic and copies ran while one was open for 0% of the time, Pallas kernels for 1%

profile of v3, /device:TPU:1, one launch (start us, length us, event | category | flops | bytes accessed | tf_op | source)
XLA Modules:
  0.0 105.0 jit_solution(8019728072779212430)
XLA Ops:
  0.6 0.9 pad_maximum_fusion
  1.6 26.0 %all_to_all.25.own_ref = bf16[32,3,8,128]{3,2,1,0:T(8,128)(2,1)S(1)} all-to-all(bf16[32,3,8,128]{3,2,1,0:T(8,128)(2,1)S(1)} %pad_maximum_fusion), channel_id=1, replica_groups=mesh['yh'=4,'yl'=2,'xl'=2,'c'=2,'z'=8,'xh'=2] {'z','xh','c'}, dimensions={0} | all-to-all | bytes 393216 | tf_op jit(solution)/shard_map/all_to_all | solution.py:203
  27.6 0.9 shard_map.85
  28.5 3.6 %all-to-all-start.1 = ((bf16[4,32,2,8,128]{4,3,2,1,0:T(8,128)(2,1)}), bf16[4,32,2,8,128]{4,3,2,1,0:T(8,128)(2,1)S(1)}, u32[]{:S(2)}, u32[]{:S(2)}) async-start(bf16[4,32,2,8,128]{4,3,2,1,0:T(8,128)(2,1)} %shard_map.85), calls=%async_computation.1 | async-start | bytes 1048576 | tf_op jit(solution)/shard_map/all_to_all | solution.py:203
  32.2 2.2 %collective-permute-start = (bf16[256,128]{1,0:T(8,128)(2,1)S(1)}, bf16[256,128]{1,0:T(8,128)(2,1)S(1)}, u32[]{:S(2)}, u32[]{:S(2)}) collective-permute-start(bf16[256,128]{1,0:T(8,128)(2,1)S(1)} %get-tuple-element.15), channel_id=1, source_target_pairs={{0,16},{16,0},{1,17},{17,1},{2,18},{18,2},{3,19},{19,3},{4,20},{20... | collective-permute-start | bytes 196616 | tf_op jit(solution)/shard_map/ppermute | solution.py:208
  34.3 1.0 collective-permute-done.got_ref
  35.3 5.9 %collective-permute-start.3 = (bf16[2,256,128]{2,1,0:T(8,128)(2,1)S(1)}, bf16[2,256,128]{2,1,0:T(8,128)(2,1)S(1)}, u32[]{:S(2)}, u32[]{:S(2)}) collective-permute-start(bf16[2,256,128]{2,1,0:T(8,128)(2,1)S(1)} %shard_map.87.kv0), channel_id=1, source_target_pairs={{0,384},{128,0},{256,128},{384,256},{1,385},{129,1},{257,129},{385... | collective-permute-start | bytes 393224 | tf_op jit(solution)/shard_map/ppermute | solution.py:208
  41.2 3.5 %collective-permute-start.2 = (bf16[2,256,128]{2,1,0:T(8,128)(2,1)S(1)}, bf16[2,256,128]{2,1,0:T(8,128)(2,1)S(1)}, u32[]{:S(2)}, u32[]{:S(2)}) collective-permute-start(bf16[2,256,128]{2,1,0:T(8,128)(2,1)S(1)} %shard_map.87.kv0), channel_id=1, source_target_pairs={{0,256},{128,384},{256,0},{384,128},{1,257},{129,385},{257,1},{385... | collective-permute-start | bytes 393224 | tf_op jit(solution)/shard_map/ppermute | solution.py:208
  44.8 4.2 %collective-permute-start.1 = (bf16[2,256,128]{2,1,0:T(8,128)(2,1)S(1)}, bf16[2,256,128]{2,1,0:T(8,128)(2,1)S(1)}, u32[]{:S(2)}, u32[]{:S(2)}) collective-permute-start(bf16[2,256,128]{2,1,0:T(8,128)(2,1)S(1)} %shard_map.87.kv0), channel_id=1, source_target_pairs={{0,128},{128,256},{256,384},{384,0},{1,129},{129,257},{257,385},{3... | collective-permute-start | bytes 393224 | tf_op jit(solution)/shard_map/ppermute | solution.py:208
  49.0 5.2 %collective-permute-done.2.kv2 = bf16[2,256,128]{2,1,0:T(8,128)(2,1)S(1)} collective-permute-done((bf16[2,256,128]{2,1,0:T(8,128)(2,1)S(1)}, bf16[2,256,128]{2,1,0:T(8,128)(2,1)S(1)}, u32[]{:S(2)}, u32[]{:S(2)}) %collective-permute-start.2) | collective-permute-done | bytes 131104 | tf_op jit(solution)/shard_map/ppermute | solution.py:208
  54.2 2.0 %shard_map.88 = f32[4,24,128]{2,1,0:T(8,128)S(1)} custom-call(s32[64]{0:T(128)S(1)} %copy-done.2, bf16[32,3,8,128]{3,2,1,0:T(8,128)(2,1)S(1)} %all_to_all.25.own_ref, bf16[4,32,2,8,128]{4,3,2,1,0:T(8,128)(2,1)S(1)} %all-to-all-done.1.q_ref, bf16[2,256,128]{2,1,0:T(8,128)(2,1)S(1)} %shard_map.87.kv0, bf16[2,256,128]{2,1,0:T(8,128)(2,1)S(1)} %collective-permute-done.1.kv1, ...), custom_call_target="tpu_custom_call" | custom-call | tf_op jit(solution)/shard_map/pallas_call | solution.py:193
  56.2 11.1 %all_to_all.26.stats_ref = f32[4,24,128]{2,1,0:T(8,128)S(1)} all-to-all(f32[4,24,128]{2,1,0:T(8,128)S(1)} %shard_map.88), channel_id=1, replica_groups=mesh['yh'=4,'yl'=2,'xl'=2,'c'=2,'z'=8,'xh'=2] {'yl','xl'}, dimensions={0} | all-to-all | bytes 98304 | tf_op jit(solution)/shard_map/all_to_all | solution.py:203
  67.3 4.2 %shard_map.89 = (bf16[4,256,128]{2,1,0:T(8,128)(2,1)}, bf16[2,256,128]{2,1,0:T(8,128)(2,1)S(1)}, bf16[2,256,128]{2,1,0:T(8,128)(2,1)S(1)}, bf16[2,256,128]{2,1,0:T(8,128)(2,1)S(1)}, bf16[2,256,128]{2,1,0:T(8,128)(2,1)S(1)}) custom-call(s32[64]{0:T(128)S(1)} %copy-done.2, f32[4,24,128]{2,1,0:T(8,128)S(1)} %all_to_all.26.stats_ref, ...), custom_call_target="tpu_custom_call" | custom-call | tf_op jit(solution)/shard_map/pallas_call | solution.py:193
  71.5 3.4 %all-to-all-start.3 = ((bf16[4,256,128]{2,1,0:T(8,128)(2,1)}), bf16[4,256,128]{2,1,0:T(8,128)(2,1)S(1)}, u32[]{:S(2)}, u32[]{:S(2)}) async-start(bf16[4,256,128]{2,1,0:T(8,128)(2,1)} %get-tuple-element.16), calls=%async_computation.3 | async-start | bytes 524288 | tf_op jit(solution)/shard_map/all_to_all | solution.py:203
  75.0 4.9 %collective-permute-start.4 = (bf16[2,256,128]{2,1,0:T(8,128)(2,1)S(1)}, bf16[2,256,128]{2,1,0:T(8,128)(2,1)S(1)}, u32[]{:S(2)}, u32[]{:S(2)}) collective-permute-start(bf16[2,256,128]{2,1,0:T(8,128)(2,1)S(1)} %get-tuple-element.18), channel_id=1, source_target_pairs={{0,384},{128,0},{256,128},{384,256},{1,385},{129,1},{257,129},{385... | collective-permute-start | bytes 393224 | tf_op jit(solution)/shard_map/ppermute | solution.py:208
  79.9 3.6 %collective-permute-start.5 = (bf16[2,256,128]{2,1,0:T(8,128)(2,1)S(1)}, bf16[2,256,128]{2,1,0:T(8,128)(2,1)S(1)}, u32[]{:S(2)}, u32[]{:S(2)}) collective-permute-start(bf16[2,256,128]{2,1,0:T(8,128)(2,1)S(1)} %get-tuple-element.19), channel_id=1, source_target_pairs={{0,256},{128,384},{256,0},{384,128},{1,257},{129,385},{257,1},{385... | collective-permute-start | bytes 393224 | tf_op jit(solution)/shard_map/ppermute | solution.py:208
  83.5 4.0 %collective-permute-start.6 = (bf16[2,256,128]{2,1,0:T(8,128)(2,1)S(1)}, bf16[2,256,128]{2,1,0:T(8,128)(2,1)S(1)}, u32[]{:S(2)}, u32[]{:S(2)}) collective-permute-start(bf16[2,256,128]{2,1,0:T(8,128)(2,1)S(1)} %get-tuple-element.20), channel_id=1, source_target_pairs={{0,128},{128,256},{256,384},{384,0},{1,129},{129,257},{257,385},{3... | collective-permute-start | bytes 393224 | tf_op jit(solution)/shard_map/ppermute | solution.py:208
  87.5 0.7 shard_map.90
  88.2 6.3 %all-to-all-start.4 = ((bf16[32,8,128]{2,1,0:T(8,128)(2,1)}), bf16[32,8,128]{2,1,0:T(8,128)(2,1)S(1)}, u32[]{:S(2)}, u32[]{:S(2)}) async-start(bf16[32,8,128]{2,1,0:T(8,128)(2,1)} %bitcast.9), calls=%async_computation.4 | async-start | bytes 131072 | tf_op jit(solution)/shard_map/all_to_all | solution.py:203
  94.7 3.2 %collective-permute-start.7 = (bf16[256,128]{1,0:T(8,128)(2,1)S(1)}, bf16[256,128]{1,0:T(8,128)(2,1)S(1)}, u32[]{:S(2)}, u32[]{:S(2)}) collective-permute-start(bf16[256,128]{1,0:T(8,128)(2,1)S(1)} %get-tuple-element.22), channel_id=1, source_target_pairs={{0,16},{16,0},{1,17},{17,1},{2,18},{18,2},{3,19},{19,3},{4,20},{20... | collective-permute-start | bytes 196616 | tf_op jit(solution)/shard_map/ppermute | solution.py:208
  97.9 0.9 collective-permute-done.7.got_ref
  98.8 0.7 shard_map.92
  99.5 4.9 %all-to-all-done.4 = bf16[32,8,128]{2,1,0:T(8,128)(2,1)S(1)} async-done(((bf16[32,8,128]{2,1,0:T(8,128)(2,1)}), bf16[32,8,128]{2,1,0:T(8,128)(2,1)S(1)}, u32[]{:S(2)}, u32[]{:S(2)}) %all-to-all-start.4) | async-done | bytes 65568 | tf_op jit(solution)/shard_map/all_to_all | solution.py:203
  104.3 0.6 copy.10
  (16 shorter events, 0.1 us)
Async XLA Ops:
  28.5 3.6 %copy-start = (bf16[128,256]{1,0:T(8,128)(2,1)S(1)}, bf16[128,256]{1,0:T(8,128)(2,1)}, u32[]{:S(2)}) copy-start(bf16[128,256]{1,0:T(8,128)(2,1)} %key_ref.1) | copy-start | bytes 196612
  28.5 3.6 %copy-start.1 = (bf16[128,256]{1,0:T(8,128)(2,1)S(1)}, bf16[128,256]{1,0:T(8,128)(2,1)}, u32[]{:S(2)}) copy-start(bf16[128,256]{1,0:T(8,128)(2,1)} %value_ref.1) | copy-start | bytes 196612
  28.5 25.7 %all-to-all-start.1 = ((bf16[4,32,2,8,128]{4,3,2,1,0:T(8,128)(2,1)}), bf16[4,32,2,8,128]{4,3,2,1,0:T(8,128)(2,1)S(1)}, u32[]{:S(2)}, u32[]{:S(2)}) async-start(bf16[4,32,2,8,128]{4,3,2,1,0:T(8,128)(2,1)} %shard_map.85), calls=%async_computation.1 | async-start | bytes 1048576 | tf_op jit(solution)/shard_map/all_to_all | solution.py:203
  32.2 3.1 %collective-permute-start = (bf16[256,128]{1,0:T(8,128)(2,1)S(1)}, bf16[256,128]{1,0:T(8,128)(2,1)S(1)}, u32[]{:S(2)}, u32[]{:S(2)}) collective-permute-start(bf16[256,128]{1,0:T(8,128)(2,1)S(1)} %get-tuple-element.15), channel_id=1, source_target_pairs={{0,16},{16,0},{1,17},{17,1},{2,18},{18,2},{3,19},{19,3},{4,20},{20... | collective-permute-start | bytes 196616 | tf_op jit(solution)/shard_map/ppermute | solution.py:208
  35.3 18.9 %copy-start.2 = (s32[64]{0:T(128)S(1)}, s32[64]{0:T(128)}, u32[]{:S(2)}) copy-start(s32[64]{0:T(128)} %place_ref.3) | copy-start | bytes 772
  35.3 13.7 %collective-permute-start.3 = (bf16[2,256,128]{2,1,0:T(8,128)(2,1)S(1)}, bf16[2,256,128]{2,1,0:T(8,128)(2,1)S(1)}, u32[]{:S(2)}, u32[]{:S(2)}) collective-permute-start(bf16[2,256,128]{2,1,0:T(8,128)(2,1)S(1)} %shard_map.87.kv0), channel_id=1, source_target_pairs={{0,384},{128,0},{256,128},{384,256},{1,385},{129,1},{257,129},{385... | collective-permute-start | bytes 393224 | tf_op jit(solution)/shard_map/ppermute | solution.py:208
  41.2 13.0 %collective-permute-start.2 = (bf16[2,256,128]{2,1,0:T(8,128)(2,1)S(1)}, bf16[2,256,128]{2,1,0:T(8,128)(2,1)S(1)}, u32[]{:S(2)}, u32[]{:S(2)}) collective-permute-start(bf16[2,256,128]{2,1,0:T(8,128)(2,1)S(1)} %shard_map.87.kv0), channel_id=1, source_target_pairs={{0,256},{128,384},{256,0},{384,128},{1,257},{129,385},{257,1},{385... | collective-permute-start | bytes 393224 | tf_op jit(solution)/shard_map/ppermute | solution.py:208
  44.8 9.4 %collective-permute-start.1 = (bf16[2,256,128]{2,1,0:T(8,128)(2,1)S(1)}, bf16[2,256,128]{2,1,0:T(8,128)(2,1)S(1)}, u32[]{:S(2)}, u32[]{:S(2)}) collective-permute-start(bf16[2,256,128]{2,1,0:T(8,128)(2,1)S(1)} %shard_map.87.kv0), channel_id=1, source_target_pairs={{0,128},{128,256},{256,384},{384,0},{1,129},{129,257},{257,385},{3... | collective-permute-start | bytes 393224 | tf_op jit(solution)/shard_map/ppermute | solution.py:208
  71.5 16.0 %all-to-all-start.3 = ((bf16[4,256,128]{2,1,0:T(8,128)(2,1)}), bf16[4,256,128]{2,1,0:T(8,128)(2,1)S(1)}, u32[]{:S(2)}, u32[]{:S(2)}) async-start(bf16[4,256,128]{2,1,0:T(8,128)(2,1)} %get-tuple-element.16), calls=%async_computation.3 | async-start | bytes 524288 | tf_op jit(solution)/shard_map/all_to_all | solution.py:203
  75.0 19.6 %collective-permute-start.4 = (bf16[2,256,128]{2,1,0:T(8,128)(2,1)S(1)}, bf16[2,256,128]{2,1,0:T(8,128)(2,1)S(1)}, u32[]{:S(2)}, u32[]{:S(2)}) collective-permute-start(bf16[2,256,128]{2,1,0:T(8,128)(2,1)S(1)} %get-tuple-element.18), channel_id=1, source_target_pairs={{0,384},{128,0},{256,128},{384,256},{1,385},{129,1},{257,129},{385... | collective-permute-start | bytes 393224 | tf_op jit(solution)/shard_map/ppermute | solution.py:208
  79.9 14.7 %collective-permute-start.5 = (bf16[2,256,128]{2,1,0:T(8,128)(2,1)S(1)}, bf16[2,256,128]{2,1,0:T(8,128)(2,1)S(1)}, u32[]{:S(2)}, u32[]{:S(2)}) collective-permute-start(bf16[2,256,128]{2,1,0:T(8,128)(2,1)S(1)} %get-tuple-element.19), channel_id=1, source_target_pairs={{0,256},{128,384},{256,0},{384,128},{1,257},{129,385},{257,1},{385... | collective-permute-start | bytes 393224 | tf_op jit(solution)/shard_map/ppermute | solution.py:208
  83.5 11.1 %collective-permute-start.6 = (bf16[2,256,128]{2,1,0:T(8,128)(2,1)S(1)}, bf16[2,256,128]{2,1,0:T(8,128)(2,1)S(1)}, u32[]{:S(2)}, u32[]{:S(2)}) collective-permute-start(bf16[2,256,128]{2,1,0:T(8,128)(2,1)S(1)} %get-tuple-element.20), channel_id=1, source_target_pairs={{0,128},{128,256},{256,384},{384,0},{1,129},{129,257},{257,385},{3... | collective-permute-start | bytes 393224 | tf_op jit(solution)/shard_map/ppermute | solution.py:208
  88.2 16.1 %all-to-all-start.4 = ((bf16[32,8,128]{2,1,0:T(8,128)(2,1)}), bf16[32,8,128]{2,1,0:T(8,128)(2,1)S(1)}, u32[]{:S(2)}, u32[]{:S(2)}) async-start(bf16[32,8,128]{2,1,0:T(8,128)(2,1)} %bitcast.9), calls=%async_computation.4 | async-start | bytes 131072 | tf_op jit(solution)/shard_map/all_to_all | solution.py:203
  94.7 4.1 %collective-permute-start.7 = (bf16[256,128]{1,0:T(8,128)(2,1)S(1)}, bf16[256,128]{1,0:T(8,128)(2,1)S(1)}, u32[]{:S(2)}, u32[]{:S(2)}) collective-permute-start(bf16[256,128]{1,0:T(8,128)(2,1)S(1)} %get-tuple-element.22), channel_id=1, source_target_pairs={{0,16},{16,0},{1,17},{17,1},{2,18},{18,2},{3,19},{19,3},{4,20},{20... | collective-permute-start | bytes 196616 | tf_op jit(solution)/shard_map/ppermute | solution.py:208

commit v4 on v3

--- a/solution.py
+++ b/solution.py
@@ -22,7 +22,7 @@
     row = lax.broadcasted_iota(jnp.int32, (SPAN, HEAD_DIM), 0)
     c = lax.axis_index("c")
     for p in range(4):
-        back = lax.rem(lax.axis_index("yh") + (4 - p), 4)
+        back = lax.axis_index("yh") ^ p
         chip = (back * 2 + lax.axis_index("yl")) * 2 + lax.axis_index("xl")
         for q in range(2):
             first = chip * 4 + (c if q == 0 else 1 - c) * 2
@@ -203,9 +203,8 @@
     return lax.all_to_all(x, axes, 0, 0, tiled=True)
 
 
-def shift(x, axis, by):
-    n = lax.axis_size(axis)
-    return lax.ppermute(x, axis, [(i, (i + by) % n) for i in range(n)])
+def swap(x, axis, bits):
+    return lax.ppermute(x, axis, [(i, i ^ bits) for i in range(lax.axis_size(axis))])
 
 
 def bf16(*shape):
@@ -219,11 +218,11 @@
         in_specs=[VMEM, VMEM],
         out_specs=(VMEM, VMEM),
     )(key_in, value_in)
-    got = shift(give, "c", 1)
+    got = swap(give, "c", 1)
     kv = kernel_call(
         join_kernel, out_shape=bf16(2, 256, HEAD_DIM), in_specs=[VMEM, VMEM], out_specs=VMEM
     )(keep, got)
-    kvs = [kv] + [shift(kv, "yh", k) for k in (1, 2, 3)]
+    kvs = [kv] + [swap(kv, "yh", k) for k in (1, 2, 3)]
 
     mine = jnp.stack([head_tiles(query_in), head_tiles(out_grad), head_tiles(out_saved)], axis=1)
     own = exchange(mine, HEADS_AXES)
@@ -252,7 +251,7 @@
         ],
     )(span_place, stats_all, q_all, *kvs)
 
-    parts = [dkvs[0]] + [shift(dkvs[k], "yh", -k) for k in (1, 2, 3)]
+    parts = [dkvs[0]] + [swap(dkvs[k], "yh", k) for k in (1, 2, 3)]
     dq_parts = exchange(dq, Q_AXES)
     dq_rows = kernel_call(
         dq_sum_kernel, out_shape=bf16(256, HEAD_DIM), in_specs=[VMEM], out_specs=VMEM
@@ -266,7 +265,7 @@
         in_specs=[VMEM] * 4,
         out_specs=(VMEM, VMEM),
     )(*parts)
-    got = shift(give, "c", 1)
+    got = swap(give, "c", 1)
     grad_key, grad_value = kernel_call(
         dkv_place_kernel,
         out_shape=(bf16(128, 256),) * 2,

time: 106 us -> 106 us (level)
  waiting for transfers between devices: 12 us -> 20.2 us
  blocking collectives: 37.2 us -> 32.3 us
  starting transfers between devices: 44.9 us -> 41.6 us
    ppermute x8, waiting for transfers between devices: 7.07 us -> 16.6 us  [swap(): lax.ppermute(x, axis, [(i, i ^ bits) for i in range(lax.axis_size(axis))])]
    all_to_all x2, blocking collectives: 37.2 us -> 32.3 us  [exchange(): return lax.all_to_all(x, axes, 0, 0, tiled=True)]
    ppermute x8, starting transfers between devices: 31.6 us -> 27.9 us  [swap(): lax.ppermute(x, axis, [(i, i ^ bits) for i in range(lax.axis_size(axis))])]
    all_to_all x3, waiting for transfers between devices: 4.89 us -> 3.62 us  [exchange(): return lax.all_to_all(x, axes, 0, 0, tiled=True)]
  transfers between devices with their start and end apart: 11 -> 11, of which waited for: 4 -> 6; matrix products, arithmetic and copies ran while one was open for 0% -> 0% of each run, Pallas kernels for 1% -> 1%
where the time goes in v4:
time: 106 us; the launch traced here: 105 us
  starting transfers between devices  41.6 us (39%)
  blocking collectives  32.3 us (30%)
  waiting for transfers between devices  20.2 us (19%)
  Pallas kernels  8.53 us (8%)
    all_to_all x2, blocking collectives, exchange(): return lax.all_to_all(x, axes, 0, 0, tiled=True)  32.3 us
    ppermute x8, starting transfers between devices, swap(): lax.ppermute(x, axis, [(i, i ^ bits) for i in range(lax.axis_size(axis))])  27.9 us
    ppermute x8, waiting for transfers between devices, swap(): lax.ppermute(x, axis, [(i, i ^ bits) for i in range(lax.axis_size(axis))])  16.6 us
    all_to_all x3, starting transfers between devices, exchange(): return lax.all_to_all(x, axes, 0, 0, tiled=True)  13.7 us
    pallas_call x8, Pallas kernels, run(): return call(*placed)  8.53 us
    all_to_all x3, waiting for transfers between devices, exchange(): return lax.all_to_all(x, axes, 0, 0, tiled=True)  3.62 us
  transfers between devices with their start and end apart: 11, of which 6 were waited for; matrix products, arithmetic and copies ran while one was open for 0% of the time, Pallas kernels for 1%

profile of v4, /device:TPU:1, one launch (start us, length us, event | category | flops | bytes accessed | tf_op | source)
XLA Modules:
  0.0 105.0 jit_solution(16855748113678958706)
XLA Ops:
  0.6 0.9 pad_maximum_fusion
  1.6 26.0 %all_to_all.25.own_ref = bf16[32,3,8,128]{3,2,1,0:T(8,128)(2,1)S(1)} all-to-all(bf16[32,3,8,128]{3,2,1,0:T(8,128)(2,1)S(1)} %pad_maximum_fusion), channel_id=1, replica_groups=mesh['yh'=4,'yl'=2,'xl'=2,'c'=2,'z'=8,'xh'=2] {'z','xh','c'}, dimensions={0} | all-to-all | bytes 393216 | tf_op jit(solution)/shard_map/all_to_all | solution.py:203
  27.6 0.9 shard_map.85
  28.5 3.6 %all-to-all-start.1 = ((bf16[4,32,2,8,128]{4,3,2,1,0:T(8,128)(2,1)}), bf16[4,32,2,8,128]{4,3,2,1,0:T(8,128)(2,1)S(1)}, u32[]{:S(2)}, u32[]{:S(2)}) async-start(bf16[4,32,2,8,128]{4,3,2,1,0:T(8,128)(2,1)} %shard_map.85), calls=%async_computation.1 | async-start | bytes 1048576 | tf_op jit(solution)/shard_map/all_to_all | solution.py:203
  32.2 2.2 %collective-permute-start = (bf16[256,128]{1,0:T(8,128)(2,1)S(1)}, bf16[256,128]{1,0:T(8,128)(2,1)S(1)}, u32[]{:S(2)}, u32[]{:S(2)}) collective-permute-start(bf16[256,128]{1,0:T(8,128)(2,1)S(1)} %get-tuple-element.15), channel_id=1, source_target_pairs={{0,16},{16,0},{1,17},{17,1},{2,18},{18,2},{3,19},{19,3},{4,20},{20... | collective-permute-start | bytes 196616 | tf_op jit(solution)/shard_map/ppermute | solution.py:207
  34.3 1.0 collective-permute-done.got_ref
  35.3 5.9 %collective-permute-start.3 = (bf16[2,256,128]{2,1,0:T(8,128)(2,1)S(1)}, bf16[2,256,128]{2,1,0:T(8,128)(2,1)S(1)}, u32[]{:S(2)}, u32[]{:S(2)}) collective-permute-start(bf16[2,256,128]{2,1,0:T(8,128)(2,1)S(1)} %shard_map.87.kv0), channel_id=1, source_target_pairs={{0,384},{128,256},{256,128},{384,0},{1,385},{129,257},{257,129},{3... | collective-permute-start | bytes 393224 | tf_op jit(solution)/shard_map/ppermute | solution.py:207
  41.2 3.5 %collective-permute-start.2 = (bf16[2,256,128]{2,1,0:T(8,128)(2,1)S(1)}, bf16[2,256,128]{2,1,0:T(8,128)(2,1)S(1)}, u32[]{:S(2)}, u32[]{:S(2)}) collective-permute-start(bf16[2,256,128]{2,1,0:T(8,128)(2,1)S(1)} %shard_map.87.kv0), channel_id=1, source_target_pairs={{0,256},{128,384},{256,0},{384,128},{1,257},{129,385},{257,1},{385... | collective-permute-start | bytes 393224 | tf_op jit(solution)/shard_map/ppermute | solution.py:207
  44.8 2.4 %collective-permute-start.1 = (bf16[2,256,128]{2,1,0:T(8,128)(2,1)S(1)}, bf16[2,256,128]{2,1,0:T(8,128)(2,1)S(1)}, u32[]{:S(2)}, u32[]{:S(2)}) collective-permute-start(bf16[2,256,128]{2,1,0:T(8,128)(2,1)S(1)} %shard_map.87.kv0), channel_id=1, source_target_pairs={{0,128},{128,0},{256,384},{384,256},{1,129},{129,1},{257,385},{385... | collective-permute-start | bytes 393224 | tf_op jit(solution)/shard_map/ppermute | solution.py:207
  47.1 8.8 %collective-permute-done.2.kv2 = bf16[2,256,128]{2,1,0:T(8,128)(2,1)S(1)} collective-permute-done((bf16[2,256,128]{2,1,0:T(8,128)(2,1)S(1)}, bf16[2,256,128]{2,1,0:T(8,128)(2,1)S(1)}, u32[]{:S(2)}, u32[]{:S(2)}) %collective-permute-start.2) | collective-permute-done | bytes 131104 | tf_op jit(solution)/shard_map/ppermute | solution.py:207
  56.0 3.8 %collective-permute-done.1.kv1 = bf16[2,256,128]{2,1,0:T(8,128)(2,1)S(1)} collective-permute-done((bf16[2,256,128]{2,1,0:T(8,128)(2,1)S(1)}, bf16[2,256,128]{2,1,0:T(8,128)(2,1)S(1)}, u32[]{:S(2)}, u32[]{:S(2)}) %collective-permute-start.1) | collective-permute-done | bytes 131104 | tf_op jit(solution)/shard_map/ppermute | solution.py:207
  59.8 2.0 %shard_map.88 = f32[4,24,128]{2,1,0:T(8,128)S(1)} custom-call(s32[64]{0:T(128)S(1)} %copy-done.2, bf16[32,3,8,128]{3,2,1,0:T(8,128)(2,1)S(1)} %all_to_all.25.own_ref, bf16[4,32,2,8,128]{4,3,2,1,0:T(8,128)(2,1)S(1)} %all-to-all-done.1.q_ref, bf16[2,256,128]{2,1,0:T(8,128)(2,1)S(1)} %shard_map.87.kv0, bf16[2,256,128]{2,1,0:T(8,128)(2,1)S(1)} %collective-permute-done.1.kv1, ...), custom_call_target="tpu_custom_call" | custom-call | tf_op jit(solution)/shard_map/pallas_call | solution.py:193
  61.8 6.3 %all_to_all.26.stats_ref = f32[4,24,128]{2,1,0:T(8,128)S(1)} all-to-all(f32[4,24,128]{2,1,0:T(8,128)S(1)} %shard_map.88), channel_id=1, replica_groups=mesh['yh'=4,'yl'=2,'xl'=2,'c'=2,'z'=8,'xh'=2] {'yl','xl'}, dimensions={0} | all-to-all | bytes 98304 | tf_op jit(solution)/shard_map/all_to_all | solution.py:203
  68.1 4.2 %shard_map.89 = (bf16[4,256,128]{2,1,0:T(8,128)(2,1)}, bf16[2,256,128]{2,1,0:T(8,128)(2,1)S(1)}, bf16[2,256,128]{2,1,0:T(8,128)(2,1)S(1)}, bf16[2,256,128]{2,1,0:T(8,128)(2,1)S(1)}, bf16[2,256,128]{2,1,0:T(8,128)(2,1)S(1)}) custom-call(s32[64]{0:T(128)S(1)} %copy-done.2, f32[4,24,128]{2,1,0:T(8,128)S(1)} %all_to_all.26.stats_ref, ...), custom_call_target="tpu_custom_call" | custom-call | tf_op jit(solution)/shard_map/pallas_call | solution.py:193
  72.3 3.4 %all-to-all-start.3 = ((bf16[4,256,128]{2,1,0:T(8,128)(2,1)}), bf16[4,256,128]{2,1,0:T(8,128)(2,1)S(1)}, u32[]{:S(2)}, u32[]{:S(2)}) async-start(bf16[4,256,128]{2,1,0:T(8,128)(2,1)} %get-tuple-element.16), calls=%async_computation.3 | async-start | bytes 524288 | tf_op jit(solution)/shard_map/all_to_all | solution.py:203
  75.7 4.4 %collective-permute-start.4 = (bf16[2,256,128]{2,1,0:T(8,128)(2,1)S(1)}, bf16[2,256,128]{2,1,0:T(8,128)(2,1)S(1)}, u32[]{:S(2)}, u32[]{:S(2)}) collective-permute-start(bf16[2,256,128]{2,1,0:T(8,128)(2,1)S(1)} %get-tuple-element.18), channel_id=1, source_target_pairs={{0,128},{128,0},{256,384},{384,256},{1,129},{129,1},{257,385},{385... | collective-permute-start | bytes 393224 | tf_op jit(solution)/shard_map/ppermute | solution.py:207
  80.1 3.3 %collective-permute-start.5 = (bf16[2,256,128]{2,1,0:T(8,128)(2,1)S(1)}, bf16[2,256,128]{2,1,0:T(8,128)(2,1)S(1)}, u32[]{:S(2)}, u32[]{:S(2)}) collective-permute-start(bf16[2,256,128]{2,1,0:T(8,128)(2,1)S(1)} %get-tuple-element.19), channel_id=1, source_target_pairs={{0,256},{128,384},{256,0},{384,128},{1,257},{129,385},{257,1},{385... | collective-permute-start | bytes 393224 | tf_op jit(solution)/shard_map/ppermute | solution.py:207
  83.3 3.9 %collective-permute-start.6 = (bf16[2,256,128]{2,1,0:T(8,128)(2,1)S(1)}, bf16[2,256,128]{2,1,0:T(8,128)(2,1)S(1)}, u32[]{:S(2)}, u32[]{:S(2)}) collective-permute-start(bf16[2,256,128]{2,1,0:T(8,128)(2,1)S(1)} %get-tuple-element.20), channel_id=1, source_target_pairs={{0,384},{128,256},{256,128},{384,0},{1,385},{129,257},{257,129},{3... | collective-permute-start | bytes 393224 | tf_op jit(solution)/shard_map/ppermute | solution.py:207
  87.9 6.7 %all-to-all-start.4 = ((bf16[32,8,128]{2,1,0:T(8,128)(2,1)}), bf16[32,8,128]{2,1,0:T(8,128)(2,1)S(1)}, u32[]{:S(2)}, u32[]{:S(2)}) async-start(bf16[32,8,128]{2,1,0:T(8,128)(2,1)} %bitcast.9), calls=%async_computation.4 | async-start | bytes 131072 | tf_op jit(solution)/shard_map/all_to_all | solution.py:203
  94.6 2.1 %collective-permute-done.6.p3 = bf16[2,256,128]{2,1,0:T(8,128)(2,1)S(1)} collective-permute-done((bf16[2,256,128]{2,1,0:T(8,128)(2,1)S(1)}, bf16[2,256,128]{2,1,0:T(8,128)(2,1)S(1)}, u32[]{:S(2)}, u32[]{:S(2)}) %collective-permute-start.6) | collective-permute-done | bytes 131104 | tf_op jit(solution)/shard_map/ppermute | solution.py:207
  96.8 2.4 %collective-permute-start.7 = (bf16[256,128]{1,0:T(8,128)(2,1)S(1)}, bf16[256,128]{1,0:T(8,128)(2,1)S(1)}, u32[]{:S(2)}, u32[]{:S(2)}) collective-permute-start(bf16[256,128]{1,0:T(8,128)(2,1)S(1)} %get-tuple-element.22), channel_id=1, source_target_pairs={{0,16},{16,0},{1,17},{17,1},{2,18},{18,2},{3,19},{19,3},{4,20},{20... | collective-permute-start | bytes 196616 | tf_op jit(solution)/shard_map/ppermute | solution.py:207
  99.2 0.9 collective-permute-done.7.got_ref
  100.1 0.7 shard_map.92
  100.8 3.6 %all-to-all-done.4 = bf16[32,8,128]{2,1,0:T(8,128)(2,1)S(1)} async-done(((bf16[32,8,128]{2,1,0:T(8,128)(2,1)}), bf16[32,8,128]{2,1,0:T(8,128)(2,1)S(1)}, u32[]{:S(2)}, u32[]{:S(2)}) %all-to-all-start.4) | async-done | bytes 65568 | tf_op jit(solution)/shard_map/all_to_all | solution.py:203
  (16 shorter events, 1.4 us)
Async XLA Ops:
  28.5 3.6 %copy-start = (bf16[128,256]{1,0:T(8,128)(2,1)S(1)}, bf16[128,256]{1,0:T(8,128)(2,1)}, u32[]{:S(2)}) copy-start(bf16[128,256]{1,0:T(8,128)(2,1)} %key_ref.1) | copy-start | bytes 196612
  28.5 3.6 %copy-start.1 = (bf16[128,256]{1,0:T(8,128)(2,1)S(1)}, bf16[128,256]{1,0:T(8,128)(2,1)}, u32[]{:S(2)}) copy-start(bf16[128,256]{1,0:T(8,128)(2,1)} %value_ref.1) | copy-start | bytes 196612
  28.5 31.3 %all-to-all-start.1 = ((bf16[4,32,2,8,128]{4,3,2,1,0:T(8,128)(2,1)}), bf16[4,32,2,8,128]{4,3,2,1,0:T(8,128)(2,1)S(1)}, u32[]{:S(2)}, u32[]{:S(2)}) async-start(bf16[4,32,2,8,128]{4,3,2,1,0:T(8,128)(2,1)} %shard_map.85), calls=%async_computation.1 | async-start | bytes 1048576 | tf_op jit(solution)/shard_map/all_to_all | solution.py:203
  32.2 3.1 %collective-permute-start = (bf16[256,128]{1,0:T(8,128)(2,1)S(1)}, bf16[256,128]{1,0:T(8,128)(2,1)S(1)}, u32[]{:S(2)}, u32[]{:S(2)}) collective-permute-start(bf16[256,128]{1,0:T(8,128)(2,1)S(1)} %get-tuple-element.15), channel_id=1, source_target_pairs={{0,16},{16,0},{1,17},{17,1},{2,18},{18,2},{3,19},{19,3},{4,20},{20... | collective-permute-start | bytes 196616 | tf_op jit(solution)/shard_map/ppermute | solution.py:207
  35.3 24.5 %copy-start.2 = (s32[64]{0:T(128)S(1)}, s32[64]{0:T(128)}, u32[]{:S(2)}) copy-start(s32[64]{0:T(128)} %place_ref.3) | copy-start | bytes 772
  35.3 11.8 %collective-permute-start.3 = (bf16[2,256,128]{2,1,0:T(8,128)(2,1)S(1)}, bf16[2,256,128]{2,1,0:T(8,128)(2,1)S(1)}, u32[]{:S(2)}, u32[]{:S(2)}) collective-permute-start(bf16[2,256,128]{2,1,0:T(8,128)(2,1)S(1)} %shard_map.87.kv0), channel_id=1, source_target_pairs={{0,384},{128,256},{256,128},{384,0},{1,385},{129,257},{257,129},{3... | collective-permute-start | bytes 393224 | tf_op jit(solution)/shard_map/ppermute | solution.py:207
  41.2 14.7 %collective-permute-start.2 = (bf16[2,256,128]{2,1,0:T(8,128)(2,1)S(1)}, bf16[2,256,128]{2,1,0:T(8,128)(2,1)S(1)}, u32[]{:S(2)}, u32[]{:S(2)}) collective-permute-start(bf16[2,256,128]{2,1,0:T(8,128)(2,1)S(1)} %shard_map.87.kv0), channel_id=1, source_target_pairs={{0,256},{128,384},{256,0},{384,128},{1,257},{129,385},{257,1},{385... | collective-permute-start | bytes 393224 | tf_op jit(solution)/shard_map/ppermute | solution.py:207
  44.8 15.0 %collective-permute-start.1 = (bf16[2,256,128]{2,1,0:T(8,128)(2,1)S(1)}, bf16[2,256,128]{2,1,0:T(8,128)(2,1)S(1)}, u32[]{:S(2)}, u32[]{:S(2)}) collective-permute-start(bf16[2,256,128]{2,1,0:T(8,128)(2,1)S(1)} %shard_map.87.kv0), channel_id=1, source_target_pairs={{0,128},{128,0},{256,384},{384,256},{1,129},{129,1},{257,385},{385... | collective-permute-start | bytes 393224 | tf_op jit(solution)/shard_map/ppermute | solution.py:207
  72.3 14.9 %all-to-all-start.3 = ((bf16[4,256,128]{2,1,0:T(8,128)(2,1)}), bf16[4,256,128]{2,1,0:T(8,128)(2,1)S(1)}, u32[]{:S(2)}, u32[]{:S(2)}) async-start(bf16[4,256,128]{2,1,0:T(8,128)(2,1)} %get-tuple-element.16), calls=%async_computation.3 | async-start | bytes 524288 | tf_op jit(solution)/shard_map/all_to_all | solution.py:203
  75.7 18.9 %collective-permute-start.4 = (bf16[2,256,128]{2,1,0:T(8,128)(2,1)S(1)}, bf16[2,256,128]{2,1,0:T(8,128)(2,1)S(1)}, u32[]{:S(2)}, u32[]{:S(2)}) collective-permute-start(bf16[2,256,128]{2,1,0:T(8,128)(2,1)S(1)} %get-tuple-element.18), channel_id=1, source_target_pairs={{0,128},{128,0},{256,384},{384,256},{1,129},{129,1},{257,385},{385... | collective-permute-start | bytes 393224 | tf_op jit(solution)/shard_map/ppermute | solution.py:207
  80.1 14.6 %collective-permute-start.5 = (bf16[2,256,128]{2,1,0:T(8,128)(2,1)S(1)}, bf16[2,256,128]{2,1,0:T(8,128)(2,1)S(1)}, u32[]{:S(2)}, u32[]{:S(2)}) collective-permute-start(bf16[2,256,128]{2,1,0:T(8,128)(2,1)S(1)} %get-tuple-element.19), channel_id=1, source_target_pairs={{0,256},{128,384},{256,0},{384,128},{1,257},{129,385},{257,1},{385... | collective-permute-start | bytes 393224 | tf_op jit(solution)/shard_map/ppermute | solution.py:207
  83.3 13.4 %collective-permute-start.6 = (bf16[2,256,128]{2,1,0:T(8,128)(2,1)S(1)}, bf16[2,256,128]{2,1,0:T(8,128)(2,1)S(1)}, u32[]{:S(2)}, u32[]{:S(2)}) collective-permute-start(bf16[2,256,128]{2,1,0:T(8,128)(2,1)S(1)} %get-tuple-element.20), channel_id=1, source_target_pairs={{0,384},{128,256},{256,128},{384,0},{1,385},{129,257},{257,129},{3... | collective-permute-start | bytes 393224 | tf_op jit(solution)/shard_map/ppermute | solution.py:207
  87.9 16.5 %all-to-all-start.4 = ((bf16[32,8,128]{2,1,0:T(8,128)(2,1)}), bf16[32,8,128]{2,1,0:T(8,128)(2,1)S(1)}, u32[]{:S(2)}, u32[]{:S(2)}) async-start(bf16[32,8,128]{2,1,0:T(8,128)(2,1)} %bitcast.9), calls=%async_computation.4 | async-start | bytes 131072 | tf_op jit(solution)/shard_map/all_to_all | solution.py:203
  96.8 3.3 %collective-permute-start.7 = (bf16[256,128]{1,0:T(8,128)(2,1)S(1)}, bf16[256,128]{1,0:T(8,128)(2,1)S(1)}, u32[]{:S(2)}, u32[]{:S(2)}) collective-permute-start(bf16[256,128]{1,0:T(8,128)(2,1)S(1)} %get-tuple-element.22), channel_id=1, source_target_pairs={{0,16},{16,0},{1,17},{17,1},{2,18},{18,2},{3,19},{19,3},{4,20},{20... | collective-permute-start | bytes 196616 | tf_op jit(solution)/shard_map/ppermute | solution.py:207

commit v5 on v4

--- a/solution.py
+++ b/solution.py
@@ -9,6 +9,7 @@
 
 HEAD_DIM = 128
 SCALE = HEAD_DIM ** (-0.5)
+LOG2_E = 1.4426950408889634
 SPAN = 64
 HEADS_AXES = ("z", "xh", "c")
 Q_AXES = ("yl", "xl")
@@ -65,10 +66,11 @@
     zeros = jnp.zeros((6, HEAD_DIM), jnp.float32)
     tops, totals = [], []
     for b in range(4):
-        scores = dot(keys, rows_of(q_ref, b, 0), ((1,), (1,))) * SCALE
+        scores = dot(keys, rows_of(q_ref, b, 0), ((1,), (1,)))
         scores = jnp.where(kpos <= query_positions(place_ref, b), scores, -jnp.inf)
-        top = jnp.maximum(jnp.max(scores, axis=0, keepdims=True), NEG)
-        total = jnp.sum(jnp.exp(scores - top), axis=0, keepdims=True)
+        top = jnp.maximum(jnp.max(scores, axis=0, keepdims=True), NEG) * SCALE
+        exps = jnp.exp2(scores * (SCALE * LOG2_E) - top * LOG2_E)
+        total = jnp.sum(exps, axis=0, keepdims=True)
         for k in range(2):
             tops.append(top[:, k * 128 : (k + 1) * 128])
             totals.append(total[:, k * 128 : (k + 1) * 128])
@@ -92,7 +94,7 @@
     total = jnp.zeros((8, HEAD_DIM), jnp.float32)
     for p in range(4):
         total += stats_ref[p, 8:16] * jnp.exp(stats_ref[p, 0:8] - top)
-    lse8 = top + jnp.log(total)
+    lse8 = (top + jnp.log(total)) * LOG2_E
     lse = jnp.concatenate([lse8[j : j + 1] for j in range(8)], axis=1)
     delta = jnp.concatenate(
         [stats_ref[b, 16 + k : 17 + k] for b in range(4) for k in range(2)], axis=1
@@ -106,8 +108,8 @@
         values = block_rows((kv0, kv1, kv2, kv3), first, step, 1)
         kpos = kpos_ref[first * 128 : (first + step) * 128, :]
         kpos = jnp.concatenate([kpos] * 8, axis=1)
-        scores = dot(keys, queries, ((1,), (1,))) * SCALE
-        probs = jnp.exp(jnp.where(kpos <= qpos, scores - lse, -jnp.inf))
+        scores = dot(keys, queries, ((1,), (1,))) * (SCALE * LOG2_E) - lse
+        probs = jnp.exp2(jnp.where(kpos <= qpos, scores, -jnp.inf))
         dprobs = dot(values, grads, ((1,), (1,)))
         dscores = (probs * (dprobs - delta) * SCALE).astype(jnp.bfloat16)
         dk = dot(dscores, queries, ((1,), (0,))).astype(jnp.bfloat16)

time: 106 us -> 106 us (level)
  no operation moved by 1% of the time
where the time goes in v5:
time: 106 us; the launch traced here: 105 us
  starting transfers between devices  41.6 us (39%)
  blocking collectives  32.3 us (30%)
  waiting for transfers between devices  20.2 us (19%)
  Pallas kernels  8.42 us (8%)
    all_to_all x2, blocking collectives, exchange(): return lax.all_to_all(x, axes, 0, 0, tiled=True)  32.3 us
    ppermute x8, starting transfers between devices, swap(): lax.ppermute(x, axis, [(i, i ^ bits) for i in range(lax.axis_size(axis))])  27.9 us
    ppermute x8, waiting for transfers between devices, swap(): lax.ppermute(x, axis, [(i, i ^ bits) for i in range(lax.axis_size(axis))])  16.6 us
    all_to_all x3, starting transfers between devices, exchange(): return lax.all_to_all(x, axes, 0, 0, tiled=True)  13.7 us
    pallas_call x8, Pallas kernels, run(): return call(*placed)  8.42 us
    all_to_all x3, waiting for transfers between devices, exchange(): return lax.all_to_all(x, axes, 0, 0, tiled=True)  3.61 us
  transfers between devices with their start and end apart: 11, of which 6 were waited for; matrix products, arithmetic and copies ran while one was open for 0% of the time, Pallas kernels for 1%

profile of v5, /device:TPU:1, one launch (start us, length us, event | category | flops | bytes accessed | tf_op | source)
XLA Modules:
  0.0 104.9 jit_solution(1712766190167242170)
XLA Ops:
  0.6 0.9 pad_maximum_fusion
  1.6 26.0 %all_to_all.25.own_ref = bf16[32,3,8,128]{3,2,1,0:T(8,128)(2,1)S(1)} all-to-all(bf16[32,3,8,128]{3,2,1,0:T(8,128)(2,1)S(1)} %pad_maximum_fusion), channel_id=1, replica_groups=mesh['yh'=4,'yl'=2,'xl'=2,'c'=2,'z'=8,'xh'=2] {'z','xh','c'}, dimensions={0} | all-to-all | bytes 393216 | tf_op jit(solution)/shard_map/all_to_all | solution.py:205
  27.6 0.9 shard_map.85
  28.5 3.6 %all-to-all-start.1 = ((bf16[4,32,2,8,128]{4,3,2,1,0:T(8,128)(2,1)}), bf16[4,32,2,8,128]{4,3,2,1,0:T(8,128)(2,1)S(1)}, u32[]{:S(2)}, u32[]{:S(2)}) async-start(bf16[4,32,2,8,128]{4,3,2,1,0:T(8,128)(2,1)} %shard_map.85), calls=%async_computation.1 | async-start | bytes 1048576 | tf_op jit(solution)/shard_map/all_to_all | solution.py:205
  32.2 2.2 %collective-permute-start = (bf16[256,128]{1,0:T(8,128)(2,1)S(1)}, bf16[256,128]{1,0:T(8,128)(2,1)S(1)}, u32[]{:S(2)}, u32[]{:S(2)}) collective-permute-start(bf16[256,128]{1,0:T(8,128)(2,1)S(1)} %get-tuple-element.15), channel_id=1, source_target_pairs={{0,16},{16,0},{1,17},{17,1},{2,18},{18,2},{3,19},{19,3},{4,20},{20... | collective-permute-start | bytes 196616 | tf_op jit(solution)/shard_map/ppermute | solution.py:209
  34.3 1.0 collective-permute-done.got_ref
  35.3 5.9 %collective-permute-start.3 = (bf16[2,256,128]{2,1,0:T(8,128)(2,1)S(1)}, bf16[2,256,128]{2,1,0:T(8,128)(2,1)S(1)}, u32[]{:S(2)}, u32[]{:S(2)}) collective-permute-start(bf16[2,256,128]{2,1,0:T(8,128)(2,1)S(1)} %shard_map.87.kv0), channel_id=1, source_target_pairs={{0,384},{128,256},{256,128},{384,0},{1,385},{129,257},{257,129},{3... | collective-permute-start | bytes 393224 | tf_op jit(solution)/shard_map/ppermute | solution.py:209
  41.2 3.5 %collective-permute-start.2 = (bf16[2,256,128]{2,1,0:T(8,128)(2,1)S(1)}, bf16[2,256,128]{2,1,0:T(8,128)(2,1)S(1)}, u32[]{:S(2)}, u32[]{:S(2)}) collective-permute-start(bf16[2,256,128]{2,1,0:T(8,128)(2,1)S(1)} %shard_map.87.kv0), channel_id=1, source_target_pairs={{0,256},{128,384},{256,0},{384,128},{1,257},{129,385},{257,1},{385... | collective-permute-start | bytes 393224 | tf_op jit(solution)/shard_map/ppermute | solution.py:209
  44.8 2.4 %collective-permute-start.1 = (bf16[2,256,128]{2,1,0:T(8,128)(2,1)S(1)}, bf16[2,256,128]{2,1,0:T(8,128)(2,1)S(1)}, u32[]{:S(2)}, u32[]{:S(2)}) collective-permute-start(bf16[2,256,128]{2,1,0:T(8,128)(2,1)S(1)} %shard_map.87.kv0), channel_id=1, source_target_pairs={{0,128},{128,0},{256,384},{384,256},{1,129},{129,1},{257,385},{385... | collective-permute-start | bytes 393224 | tf_op jit(solution)/shard_map/ppermute | solution.py:209
  47.1 8.8 %collective-permute-done.2.kv2 = bf16[2,256,128]{2,1,0:T(8,128)(2,1)S(1)} collective-permute-done((bf16[2,256,128]{2,1,0:T(8,128)(2,1)S(1)}, bf16[2,256,128]{2,1,0:T(8,128)(2,1)S(1)}, u32[]{:S(2)}, u32[]{:S(2)}) %collective-permute-start.2) | collective-permute-done | bytes 131104 | tf_op jit(solution)/shard_map/ppermute | solution.py:209
  56.0 3.8 %collective-permute-done.1.kv1 = bf16[2,256,128]{2,1,0:T(8,128)(2,1)S(1)} collective-permute-done((bf16[2,256,128]{2,1,0:T(8,128)(2,1)S(1)}, bf16[2,256,128]{2,1,0:T(8,128)(2,1)S(1)}, u32[]{:S(2)}, u32[]{:S(2)}) %collective-permute-start.1) | collective-permute-done | bytes 131104 | tf_op jit(solution)/shard_map/ppermute | solution.py:209
  59.8 2.1 %shard_map.88 = f32[4,24,128]{2,1,0:T(8,128)S(1)} custom-call(s32[64]{0:T(128)S(1)} %copy-done.2, bf16[32,3,8,128]{3,2,1,0:T(8,128)(2,1)S(1)} %all_to_all.25.own_ref, bf16[4,32,2,8,128]{4,3,2,1,0:T(8,128)(2,1)S(1)} %all-to-all-done.1.q_ref, bf16[2,256,128]{2,1,0:T(8,128)(2,1)S(1)} %shard_map.87.kv0, bf16[2,256,128]{2,1,0:T(8,128)(2,1)S(1)} %collective-permute-done.1.kv1, ...), custom_call_target="tpu_custom_call" | custom-call | tf_op jit(solution)/shard_map/pallas_call | solution.py:195
  61.9 6.3 %all_to_all.26.stats_ref = f32[4,24,128]{2,1,0:T(8,128)S(1)} all-to-all(f32[4,24,128]{2,1,0:T(8,128)S(1)} %shard_map.88), channel_id=1, replica_groups=mesh['yh'=4,'yl'=2,'xl'=2,'c'=2,'z'=8,'xh'=2] {'yl','xl'}, dimensions={0} | all-to-all | bytes 98304 | tf_op jit(solution)/shard_map/all_to_all | solution.py:205
  68.1 4.0 %shard_map.89 = (bf16[4,256,128]{2,1,0:T(8,128)(2,1)}, bf16[2,256,128]{2,1,0:T(8,128)(2,1)S(1)}, bf16[2,256,128]{2,1,0:T(8,128)(2,1)S(1)}, bf16[2,256,128]{2,1,0:T(8,128)(2,1)S(1)}, bf16[2,256,128]{2,1,0:T(8,128)(2,1)S(1)}) custom-call(s32[64]{0:T(128)S(1)} %copy-done.2, f32[4,24,128]{2,1,0:T(8,128)S(1)} %all_to_all.26.stats_ref, ...), custom_call_target="tpu_custom_call" | custom-call | tf_op jit(solution)/shard_map/pallas_call | solution.py:195
  72.2 3.4 %all-to-all-start.3 = ((bf16[4,256,128]{2,1,0:T(8,128)(2,1)}), bf16[4,256,128]{2,1,0:T(8,128)(2,1)S(1)}, u32[]{:S(2)}, u32[]{:S(2)}) async-start(bf16[4,256,128]{2,1,0:T(8,128)(2,1)} %get-tuple-element.16), calls=%async_computation.3 | async-start | bytes 524288 | tf_op jit(solution)/shard_map/all_to_all | solution.py:205
  75.6 4.4 %collective-permute-start.4 = (bf16[2,256,128]{2,1,0:T(8,128)(2,1)S(1)}, bf16[2,256,128]{2,1,0:T(8,128)(2,1)S(1)}, u32[]{:S(2)}, u32[]{:S(2)}) collective-permute-start(bf16[2,256,128]{2,1,0:T(8,128)(2,1)S(1)} %get-tuple-element.18), channel_id=1, source_target_pairs={{0,128},{128,0},{256,384},{384,256},{1,129},{129,1},{257,385},{385... | collective-permute-start | bytes 393224 | tf_op jit(solution)/shard_map/ppermute | solution.py:209
  79.9 3.3 %collective-permute-start.5 = (bf16[2,256,128]{2,1,0:T(8,128)(2,1)S(1)}, bf16[2,256,128]{2,1,0:T(8,128)(2,1)S(1)}, u32[]{:S(2)}, u32[]{:S(2)}) collective-permute-start(bf16[2,256,128]{2,1,0:T(8,128)(2,1)S(1)} %get-tuple-element.19), channel_id=1, source_target_pairs={{0,256},{128,384},{256,0},{384,128},{1,257},{129,385},{257,1},{385... | collective-permute-start | bytes 393224 | tf_op jit(solution)/shard_map/ppermute | solution.py:209
  83.2 3.8 %collective-permute-start.6 = (bf16[2,256,128]{2,1,0:T(8,128)(2,1)S(1)}, bf16[2,256,128]{2,1,0:T(8,128)(2,1)S(1)}, u32[]{:S(2)}, u32[]{:S(2)}) collective-permute-start(bf16[2,256,128]{2,1,0:T(8,128)(2,1)S(1)} %get-tuple-element.20), channel_id=1, source_target_pairs={{0,384},{128,256},{256,128},{384,0},{1,385},{129,257},{257,129},{3... | collective-permute-start | bytes 393224 | tf_op jit(solution)/shard_map/ppermute | solution.py:209
  87.8 6.7 %all-to-all-start.4 = ((bf16[32,8,128]{2,1,0:T(8,128)(2,1)}), bf16[32,8,128]{2,1,0:T(8,128)(2,1)S(1)}, u32[]{:S(2)}, u32[]{:S(2)}) async-start(bf16[32,8,128]{2,1,0:T(8,128)(2,1)} %bitcast.9), calls=%async_computation.4 | async-start | bytes 131072 | tf_op jit(solution)/shard_map/all_to_all | solution.py:205
  94.5 2.1 %collective-permute-done.6.p3 = bf16[2,256,128]{2,1,0:T(8,128)(2,1)S(1)} collective-permute-done((bf16[2,256,128]{2,1,0:T(8,128)(2,1)S(1)}, bf16[2,256,128]{2,1,0:T(8,128)(2,1)S(1)}, u32[]{:S(2)}, u32[]{:S(2)}) %collective-permute-start.6) | collective-permute-done | bytes 131104 | tf_op jit(solution)/shard_map/ppermute | solution.py:209
  96.7 2.4 %collective-permute-start.7 = (bf16[256,128]{1,0:T(8,128)(2,1)S(1)}, bf16[256,128]{1,0:T(8,128)(2,1)S(1)}, u32[]{:S(2)}, u32[]{:S(2)}) collective-permute-start(bf16[256,128]{1,0:T(8,128)(2,1)S(1)} %get-tuple-element.22), channel_id=1, source_target_pairs={{0,16},{16,0},{1,17},{17,1},{2,18},{18,2},{3,19},{19,3},{4,20},{20... | collective-permute-start | bytes 196616 | tf_op jit(solution)/shard_map/ppermute | solution.py:209
  99.1 0.9 collective-permute-done.7.got_ref
  100.0 0.7 shard_map.92
  100.7 3.6 %all-to-all-done.4 = bf16[32,8,128]{2,1,0:T(8,128)(2,1)S(1)} async-done(((bf16[32,8,128]{2,1,0:T(8,128)(2,1)}), bf16[32,8,128]{2,1,0:T(8,128)(2,1)S(1)}, u32[]{:S(2)}, u32[]{:S(2)}) %all-to-all-start.4) | async-done | bytes 65568 | tf_op jit(solution)/shard_map/all_to_all | solution.py:205
  (16 shorter events, 1.4 us)
Async XLA Ops:
  28.5 3.6 %copy-start = (bf16[128,256]{1,0:T(8,128)(2,1)S(1)}, bf16[128,256]{1,0:T(8,128)(2,1)}, u32[]{:S(2)}) copy-start(bf16[128,256]{1,0:T(8,128)(2,1)} %key_ref.1) | copy-start | bytes 196612
  28.5 3.6 %copy-start.1 = (bf16[128,256]{1,0:T(8,128)(2,1)S(1)}, bf16[128,256]{1,0:T(8,128)(2,1)}, u32[]{:S(2)}) copy-start(bf16[128,256]{1,0:T(8,128)(2,1)} %value_ref.1) | copy-start | bytes 196612
  28.5 31.3 %all-to-all-start.1 = ((bf16[4,32,2,8,128]{4,3,2,1,0:T(8,128)(2,1)}), bf16[4,32,2,8,128]{4,3,2,1,0:T(8,128)(2,1)S(1)}, u32[]{:S(2)}, u32[]{:S(2)}) async-start(bf16[4,32,2,8,128]{4,3,2,1,0:T(8,128)(2,1)} %shard_map.85), calls=%async_computation.1 | async-start | bytes 1048576 | tf_op jit(solution)/shard_map/all_to_all | solution.py:205
  32.2 3.1 %collective-permute-start = (bf16[256,128]{1,0:T(8,128)(2,1)S(1)}, bf16[256,128]{1,0:T(8,128)(2,1)S(1)}, u32[]{:S(2)}, u32[]{:S(2)}) collective-permute-start(bf16[256,128]{1,0:T(8,128)(2,1)S(1)} %get-tuple-element.15), channel_id=1, source_target_pairs={{0,16},{16,0},{1,17},{17,1},{2,18},{18,2},{3,19},{19,3},{4,20},{20... | collective-permute-start | bytes 196616 | tf_op jit(solution)/shard_map/ppermute | solution.py:209
  35.3 24.5 %copy-start.2 = (s32[64]{0:T(128)S(1)}, s32[64]{0:T(128)}, u32[]{:S(2)}) copy-start(s32[64]{0:T(128)} %place_ref.3) | copy-start | bytes 772
  35.3 11.8 %collective-permute-start.3 = (bf16[2,256,128]{2,1,0:T(8,128)(2,1)S(1)}, bf16[2,256,128]{2,1,0:T(8,128)(2,1)S(1)}, u32[]{:S(2)}, u32[]{:S(2)}) collective-permute-start(bf16[2,256,128]{2,1,0:T(8,128)(2,1)S(1)} %shard_map.87.kv0), channel_id=1, source_target_pairs={{0,384},{128,256},{256,128},{384,0},{1,385},{129,257},{257,129},{3... | collective-permute-start | bytes 393224 | tf_op jit(solution)/shard_map/ppermute | solution.py:209
  41.2 14.7 %collective-permute-start.2 = (bf16[2,256,128]{2,1,0:T(8,128)(2,1)S(1)}, bf16[2,256,128]{2,1,0:T(8,128)(2,1)S(1)}, u32[]{:S(2)}, u32[]{:S(2)}) collective-permute-start(bf16[2,256,128]{2,1,0:T(8,128)(2,1)S(1)} %shard_map.87.kv0), channel_id=1, source_target_pairs={{0,256},{128,384},{256,0},{384,128},{1,257},{129,385},{257,1},{385... | collective-permute-start | bytes 393224 | tf_op jit(solution)/shard_map/ppermute | solution.py:209
  44.8 15.0 %collective-permute-start.1 = (bf16[2,256,128]{2,1,0:T(8,128)(2,1)S(1)}, bf16[2,256,128]{2,1,0:T(8,128)(2,1)S(1)}, u32[]{:S(2)}, u32[]{:S(2)}) collective-permute-start(bf16[2,256,128]{2,1,0:T(8,128)(2,1)S(1)} %shard_map.87.kv0), channel_id=1, source_target_pairs={{0,128},{128,0},{256,384},{384,256},{1,129},{129,1},{257,385},{385... | collective-permute-start | bytes 393224 | tf_op jit(solution)/shard_map/ppermute | solution.py:209
  72.2 14.9 %all-to-all-start.3 = ((bf16[4,256,128]{2,1,0:T(8,128)(2,1)}), bf16[4,256,128]{2,1,0:T(8,128)(2,1)S(1)}, u32[]{:S(2)}, u32[]{:S(2)}) async-start(bf16[4,256,128]{2,1,0:T(8,128)(2,1)} %get-tuple-element.16), calls=%async_computation.3 | async-start | bytes 524288 | tf_op jit(solution)/shard_map/all_to_all | solution.py:205
  75.6 18.9 %collective-permute-start.4 = (bf16[2,256,128]{2,1,0:T(8,128)(2,1)S(1)}, bf16[2,256,128]{2,1,0:T(8,128)(2,1)S(1)}, u32[]{:S(2)}, u32[]{:S(2)}) collective-permute-start(bf16[2,256,128]{2,1,0:T(8,128)(2,1)S(1)} %get-tuple-element.18), channel_id=1, source_target_pairs={{0,128},{128,0},{256,384},{384,256},{1,129},{129,1},{257,385},{385... | collective-permute-start | bytes 393224 | tf_op jit(solution)/shard_map/ppermute | solution.py:209
  79.9 14.6 %collective-permute-start.5 = (bf16[2,256,128]{2,1,0:T(8,128)(2,1)S(1)}, bf16[2,256,128]{2,1,0:T(8,128)(2,1)S(1)}, u32[]{:S(2)}, u32[]{:S(2)}) collective-permute-start(bf16[2,256,128]{2,1,0:T(8,128)(2,1)S(1)} %get-tuple-element.19), channel_id=1, source_target_pairs={{0,256},{128,384},{256,0},{384,128},{1,257},{129,385},{257,1},{385... | collective-permute-start | bytes 393224 | tf_op jit(solution)/shard_map/ppermute | solution.py:209
  83.2 13.4 %collective-permute-start.6 = (bf16[2,256,128]{2,1,0:T(8,128)(2,1)S(1)}, bf16[2,256,128]{2,1,0:T(8,128)(2,1)S(1)}, u32[]{:S(2)}, u32[]{:S(2)}) collective-permute-start(bf16[2,256,128]{2,1,0:T(8,128)(2,1)S(1)} %get-tuple-element.20), channel_id=1, source_target_pairs={{0,384},{128,256},{256,128},{384,0},{1,385},{129,257},{257,129},{3... | collective-permute-start | bytes 393224 | tf_op jit(solution)/shard_map/ppermute | solution.py:209
  87.8 16.5 %all-to-all-start.4 = ((bf16[32,8,128]{2,1,0:T(8,128)(2,1)}), bf16[32,8,128]{2,1,0:T(8,128)(2,1)S(1)}, u32[]{:S(2)}, u32[]{:S(2)}) async-start(bf16[32,8,128]{2,1,0:T(8,128)(2,1)} %bitcast.9), calls=%async_computation.4 | async-start | bytes 131072 | tf_op jit(solution)/shard_map/all_to_all | solution.py:205
  96.7 3.3 %collective-permute-start.7 = (bf16[256,128]{1,0:T(8,128)(2,1)S(1)}, bf16[256,128]{1,0:T(8,128)(2,1)S(1)}, u32[]{:S(2)}, u32[]{:S(2)}) collective-permute-start(bf16[256,128]{1,0:T(8,128)(2,1)S(1)} %get-tuple-element.22), channel_id=1, source_target_pairs={{0,16},{16,0},{1,17},{17,1},{2,18},{18,2},{3,19},{19,3},{4,20},{20... | collective-permute-start | bytes 196616 | tf_op jit(solution)/shard_map/ppermute | solution.py:209
